TPU v7x, 256 devices: a whole 4x4x8 slice. The times are simulated.
256 devices in a mesh: rep: 2 (over core), dp: 128 (over x, y, z).
Axes of the slice: x: 4, y: 4, z: 8, core: 2. Of those that a mesh axis runs over, the one named last changes fastest.
Arguments:
- x: bfloat16 [256, 2048, 1024], P(('rep', 'dp')), parts along dimension 0
- dy: bfloat16 [256, 2048, 1024], P(('rep', 'dp')), parts along dimension 0
- w_gate: bfloat16 [2, 1024, 2816], replicated
- w_up: bfloat16 [2, 1024, 2816], replicated
- w_down: bfloat16 [2, 2816, 1024], replicated
- m_w_gate: float32 [2, 1024, 2816], P(None, 'dp')
- m_w_up: float32 [2, 1024, 2816], P(None, 'dp')
- m_w_down: float32 [2, 2816, 1024], P(None, 'dp')
- v_w_gate: float32 [2, 1024, 2816], P(None, 'dp')
- v_w_up: float32 [2, 1024, 2816], P(None, 'dp')
- v_w_down: float32 [2, 2816, 1024], P(None, 'dp')
Outputs:
- output 1: bfloat16 [4, 1024, 2816], P('rep'), parts along dimension 0
- output 2: bfloat16 [4, 1024, 2816], P('rep'), parts along dimension 0
- output 3: bfloat16 [4, 2816, 1024], P('rep'), parts along dimension 0
- output 4: float32 [4, 1024, 2816], P('rep', 'dp'), parts along dimension 0
- output 5: float32 [4, 1024, 2816], P('rep', 'dp'), parts along dimension 0
- output 6: float32 [4, 2816, 1024], P('rep', 'dp'), parts along dimension 0
- output 7: float32 [4, 1024, 2816], P('rep', 'dp'), parts along dimension 0
- output 8: float32 [4, 1024, 2816], P('rep', 'dp'), parts along dimension 0
- output 9: float32 [4, 2816, 1024], P('rep', 'dp'), parts along dimension 0
There are 2 independent parts. A program takes and returns all parts, laid end to end along the dimension named above; an argument that names none is the same for every part.
All inputs are finite; a program needn't handle non-finite values.
Results may differ from a plain program's by a relative error of at most 0.022.
Values are sent between devices in bfloat16 or wider.
A program may use at most 768 MiB of HBM per device.

v0:
```python
import jax
import jax.numpy as jnp
from jax import lax

NAMES = ("w_gate", "w_up", "w_down")


def matmul(a, w):
    return jnp.dot(a, w, preferred_element_type=jnp.float32).astype(jnp.bfloat16)


def normed(h):
    wide = h.astype(jnp.float32)
    scale = lax.rsqrt(jnp.mean(wide**2, -1, keepdims=True) + 1e-6)
    return (wide * scale).astype(jnp.bfloat16)


def layer(h, w):
    a = normed(h)
    gate = jnp.dot(a, w["w_gate"], preferred_element_type=jnp.float32)
    up = jnp.dot(a, w["w_up"], preferred_element_type=jnp.float32)
    return h + matmul((jax.nn.silu(gate) * up).astype(jnp.bfloat16), w["w_down"])


def adamw(w, m, v, g):
    m = 0.9 * m + 0.1 * g
    v = 0.95 * v + 0.05 * g * g
    step = m * lax.rsqrt(v + 1e-8) + 0.1 * w
    return (w - 0.02 * step).astype(jnp.bfloat16), m, v


def stack(weights, h):
    for number in range(weights["w_gate"].shape[0]):
        h = layer(h, {name: w[number] for name, w in weights.items()})
    return h


def solution(mesh):
    groups = mesh.shape["rep"]

    def step(x, dy, *arrays):
        weights, m, v = (arrays[i : i + 3] for i in (0, 3, 6))
        x, dy = (t.reshape(groups, -1, *t.shape[1:]) for t in (x, dy))

        def of_a_group(x, dy):
            _, back = jax.vjp(lambda w: stack(w, x), dict(zip(NAMES, weights, strict=True)))
            by_weights = back(dy)[0]
            gradients = [by_weights[name].astype(jnp.float32) for name in NAMES]
            new = [adamw(w.astype(jnp.float32), m, v, g) for w, m, v, g in zip(weights, m, v, gradients, strict=True)]
            return tuple(one[which] for which in range(3) for one in new)

        return tuple(t.reshape(-1, *t.shape[2:]) for t in jax.vmap(of_a_group)(x, dy))

    return step
```

profile of v0, /device:TPU:1, one launch (start us, length us, event | category | flops | bytes accessed | tf_op | source)
XLA Modules:
  0.0 3507.0 jit_solution(11590399242069272680)
XLA Ops:
  10.3 6.6 copy.6
  16.9 20.0 fusion.69
  36.9 18.2 fusion.67
  55.1 19.6 fusion.28
  74.7 19.6 fusion.41
  94.9 20.4 fusion.58
  115.4 18.4 fusion.61
  133.8 17.1 convolution_convert_fusion.1
  150.9 19.5 fusion.8
  174.8 14.8 convolution_bitcast_fusion.1
  189.7 6.5 copy.7
  196.3 20.1 fusion.26
  216.4 19.2 fusion.43
  235.6 6.1 fusion.83
  241.7 18.8 convolution_convert_fusion
  260.6 26.0 fusion.53
  286.6 23.9 fusion.44
  310.6 23.4 fusion.47
  334.1 19.2 convolution_bitcast_fusion
  353.3 24.3 fusion.50
  377.7 434.7 %fusion.133 = (f32[24,1024]{1,0:T(8,128)S(1)}, f32[24,1024]{1,0:T(8,128)S(1)}) fusion(f32[1,2816,1024]{2,1,0:T(8,128)} %convolution_bitcast_fusion, f32[1,2816,1024]{2,1,0:T(8,128)} %fusion.50), kind=kCustom, calls=%all-reduce-scatter.2 | all-reduce-scatter fusion | flops 6291457 | bytes 23266304
  828.8 15.2 collective-permute-start.8
  864.3 5.7 collective-permute-start.16
  877.0 10.3 collective-permute-start.20
  899.5 650.5 %reduce-scatter.23.cloned.1.call-done = f32[1,8,2816]{2,1,0:T(8,128)} async-done(((f32[1,1024,2816]{2,1,0:T(8,128)}), f32[1,8,2816]{2,1,0:T(8,128)}) %reduce-scatter.23.cloned.1.call-update) | async-done | bytes 90128
  1552.8 716.6 %reduce-scatter.25.cloned.1.call-done = f32[1,8,2816]{2,1,0:T(8,128)} async-done(((f32[1,1024,2816]{2,1,0:T(8,128)}), f32[1,8,2816]{2,1,0:T(8,128)}) %reduce-scatter.25.cloned.1.call-update) | async-done | bytes 90128
  2270.3 716.2 %reduce-scatter.27.cloned.1.call-done = f32[1,8,2816]{2,1,0:T(8,128)} async-done(((f32[1,1024,2816]{2,1,0:T(8,128)}), f32[1,8,2816]{2,1,0:T(8,128)}) %reduce-scatter.27.cloned.1.call-update) | async-done | bytes 90128
  2990.8 224.0 %all-gather.14.cloned.1.call-done = bf16[1,2,2816,1024]{3,1,0,2:T(2,128)(2,1)} async-done(((bf16[1,2,22,1024]{3,1,0,2:T(2,128)(2,1)}), bf16[1,2,2816,1024]{3,1,0,2:T(2,128)(2,1)}) %all-gather.14.cloned.1.call-update) | async-done | bytes 11534352 | tf_op jit(solution)/reshape | solution.py:52
  3214.8 11.8 copy.11
  3226.6 122.2 %all-gather.10.cloned.1.call-done = bf16[1,2,1024,2816]{3,2,1,0:T(8,128)(2,1)} async-done(((bf16[1,2,8,2816]{3,2,1,0:T(8,128)(2,1)}), bf16[1,2,1024,2816]{3,2,1,0:T(8,128)(2,1)}) %all-gather.10.cloned.1.call-update) | async-done | bytes 11534352 | tf_op jit(solution)/reshape | solution.py:52
  3348.8 134.5 %all-gather.12.cloned.1.call-done = bf16[1,2,1024,2816]{3,2,1,0:T(8,128)(2,1)} async-done(((bf16[1,2,8,2816]{3,2,1,0:T(8,128)(2,1)}), bf16[1,2,1024,2816]{3,2,1,0:T(8,128)(2,1)}) %all-gather.12.cloned.1.call-update) | async-done | bytes 11534352 | tf_op jit(solution)/reshape | solution.py:52
  3483.4 10.4 copy.34
  (121 shorter events, 76.4 us)
Async XLA Ops:
  7.2 891.4 %reduce-scatter.21.cloned.1.call-start = ((), (), s32[]{:S(2)}) async-start(), calls=%async_computation.7 | async-start | bytes 11624448
  189.7 1360.4 %reduce-scatter.23.cloned.1.call-start = ((), (), s32[]{:S(2)}) async-start(), calls=%async_computation.8 | async-start | bytes 11624448
  286.6 1982.8 %reduce-scatter.25.cloned.1.call-start = ((), (), s32[]{:S(2)}) async-start(), calls=%async_computation.9 | async-start | bytes 11624448
  310.6 2676.0 %reduce-scatter.27.cloned.1.call-start = ((), (), s32[]{:S(2)}) async-start(), calls=%async_computation.10 | async-start | bytes 11624448
  334.0 2880.8 %all-gather.14.cloned.1.call-start = ((), (), s32[]{:S(2)}) async-start(), calls=%async_computation.6 | async-start | bytes 11624448 | tf_op jit(solution)/reshape | solution.py:52
  377.7 1173.3 %copy-start.9 = (f32[2,8,2816]{2,1,0:T(8,128)S(1)}, f32[2,8,2816]{2,1,0:T(8,128)}, u32[]{:S(2)}) copy-start(f32[2,8,2816]{2,1,0:T(8,128)} %param.6) | copy-start | bytes 540676
  377.7 2609.7 %copy-start.11 = (f32[2,8,2816]{2,1,0:T(8,128)S(1)}, f32[2,8,2816]{2,1,0:T(8,128)}, u32[]{:S(2)}) copy-start(f32[2,8,2816]{2,1,0:T(8,128)} %param.8) | copy-start | bytes 540676
  377.7 2609.7 %copy-start.12 = (f32[2,8,2816]{2,1,0:T(8,128)S(1)}, f32[2,8,2816]{2,1,0:T(8,128)}, u32[]{:S(2)}) copy-start(f32[2,8,2816]{2,1,0:T(8,128)} %param.7) | copy-start | bytes 540676
  812.5 6.5 collective-permute-start.10
  813.8 8.6 collective-permute-start.21
  815.1 11.0 collective-permute-start.1
  816.4 11.0 collective-permute-start.2
  817.7 11.1 collective-permute-start.3
  819.0 25.0 collective-permute-start.4
  822.4 22.9 collective-permute-start.5
  826.1 23.0 collective-permute-start.6
  827.4 25.6 collective-permute-start.7
  828.8 28.1 collective-permute-start.8
  844.0 16.2 collective-permute-start.9
  845.3 19.0 collective-permute-start
  849.1 20.9 collective-permute-start.12
  853.1 20.0 collective-permute-start.13
  856.8 18.0 collective-permute-start.14
  860.2 16.8 collective-permute-start.15
  864.3 23.0 collective-permute-start.16
  870.0 24.7 collective-permute-start.17
  873.1 21.6 collective-permute-start.18
  874.8 19.9 collective-permute-start.19
  877.0 17.7 collective-permute-start.20
  887.3 7.4 collective-permute-start.11
  898.5 2450.3 %all-gather.10.cloned.1.call-start = ((), (), s32[]{:S(2)}) async-start(), calls=%async_computation.4 | async-start | bytes 11624448 | tf_op jit(solution)/reshape | solution.py:52
  1552.7 1930.6 %all-gather.12.cloned.1.call-start = ((), (), s32[]{:S(2)}) async-start(), calls=%async_computation.5 | async-start | bytes 11624448 | tf_op jit(solution)/reshape | solution.py:52
  (17 other events, 2935.6 us)
Sparse Core Ops, SparseCore 0:
  189.8 651.5 reduce-scatter.20
  844.0 706.0 reduce-scatter.22
  1552.6 716.7 reduce-scatter.24
  2272.3 714.1 reduce-scatter.26
  2990.4 224.3 all-gather.13
  3218.8 130.0 all-gather.9
  3352.9 130.4 all-gather.11
where the time goes:
time: 3510 us
  waiting for transfers between devices  2560 us (73%)
  blocking collectives  435 us (12%)
  matrix products  304 us (9%)
  starting transfers between devices  78.2 us (2%)
  other arithmetic  56.5 us (2%)
  local copies, waits for them, and re-layouts  53.2 us (2%)
    unnamed x33, waiting for transfers between devices  2080 us
    reshape x3, waiting for transfers between devices, step(): t.reshape(-1, *t.shape[2:])  481 us
    unnamed x1, blocking collectives  435 us
    dot_general x5, matrix products, layer(): up = jnp.dot(a, w['w_up'], preferred_element_type=jnp.float32)  104 us
    dot_general x5, matrix products, layer(): gate = jnp.dot(a, w['w_gate'], preferred_element_type=jnp.float32)  100 us
    dot_general x5, matrix products, matmul(): jnp.dot(a, w, preferred_element_type=jnp.float32).astype(jnp.bfloat16)  99.1 us
    unnamed x26, starting transfers between devices  78 us
  transfers between devices with their start and end apart: 29, of which 6 were waited for; matrix products, arithmetic and copies ran while one was open for 19% of the time, Pallas kernels for 0%

commit v1 on v0

v1 whole, which is shorter than its diff:
```python
import functools

import jax
import jax.numpy as jnp
from jax import lax
from jax.experimental import pallas as pl
from jax.experimental.pallas import tpu as pltpu

LOGICAL = pl.DeviceIdType.LOGICAL
F32, BF16 = jnp.float32, jnp.bfloat16
T, D, FF = 2048, 1024, 2816
SIZE = {"x": 4, "y": 4, "z": 8}
STRIDE = {"x": 32, "y": 8, "z": 1}
PARTNERS = 13
MESSAGES = 39


class Place:
    def __init__(self):
        me = lax.axis_index("dp")
        self.at = {"x": me // 32, "y": (me // 8) % 4, "z": me % 8}
        self.number = lax.axis_index("rep") * 128 + me
        self.ring = {(axis, step): (self.at_step(axis, step), self.partner(axis, step)) for axis in "xyz" for step in (1, -1)}

    def at_step(self, axis, step):
        return lax.rem(self.at[axis] + (step + SIZE[axis] if isinstance(step, int) else step), SIZE[axis])

    def chunk(self, axis, step):
        return self.at[axis] if isinstance(step, int) and step == 0 else self.at_step(axis, step)

    def partner(self, axis, step):
        return self.number + (self.at_step(axis, step) - self.at[axis]) * STRIDE[axis]

    def tell(self, semaphore):
        for axis, n in SIZE.items():

            def one(step, c, axis=axis):
                pl.semaphore_signal(semaphore, inc=1, device_id=self.partner(axis, step), device_id_type=LOGICAL)
                return c

            lax.fori_loop(1, n, one, 0)

    def greet(self):
        barrier = pltpu.get_barrier_semaphore()
        self.tell(barrier)
        pl.semaphore_wait(barrier, PARTNERS)


class Action:
    def __init__(self, waits, do, sends, cost=0.3, frees=False):
        self.waits, self.do, self.sends, self.cost, self.frees = waits, do, sends, cost, frees


class Chain:
    def __init__(self, actions, release, before=None):
        self.actions, self.release, self.before, self.done, self.freed = actions, release, before, 0, None

    def ended(self):
        return self.done == len(self.actions)


RATE = 46.0e3


def plan(chains, ticks, latency=3.0):
    free, arrive, now, placed, rest = {}, {}, 0.0, [], []

    def run(c, a, at):
        if a.frees:
            c.freed = at
        for name, link, nbytes, further in a.sends:
            begin = max(free.get(link, 0.0), at + a.cost)
            free[link] = begin + nbytes / RATE
            arrive[name] = free[link] + latency + further

    def ready(c, tick):
        if c.ended() or c.release > tick or (c.before and c.before.freed is None):
            return None
        waits = c.actions[c.done].waits
        known = [arrive[w] for w in waits if w in arrive] + [c.before.freed + latency if c.before else 0.0]
        return max(known) if len(known) > len(waits) else None

    for tick, time in enumerate(ticks):
        now += time
        here = []
        while True:
            best = min(((r, i) for i, c in enumerate(chains) if (r := ready(c, tick)) is not None and r <= now), default=None)
            if best is None:
                break
            c = chains[best[1]]
            a = c.actions[c.done]
            c.done += 1
            run(c, a, now)
            now += a.cost
            here.append(a)
        placed.append(here)
    while not all(c.ended() for c in chains):
        r, i = min((max(r, now - 1e3), i) for i, c in enumerate(chains) if (r := ready(c, len(ticks))) is not None)
        c = chains[i]
        a = c.actions[c.done]
        c.done += 1
        now = max(r, now)
        run(c, a, now)
        now += a.cost
        rest.append(a)
    return placed, rest, now


def volume(shape):
    n = 2
    for v in shape:
        n *= v
    return n


def each(shape, f):
    if len(shape) > 3 or shape[-2] == 176 and len(shape) == 3:
        lax.fori_loop(0, shape[0], lambda i, c: (f((i,)), c)[1], 0)
    else:
        f((slice(None),) * len(shape))


class Strip:
    def __init__(self, kind, start, width, role, axes):
        self.kind, self.start, self.width, self.role, self.axes = kind, start, width, role, axes
        self.cols = pl.ds(start, width)
        left = [a for a in "xyz" if a != axes[0]]
        if kind == "down":
            shapes = ((4, 176), (176,), (24,))
        else:
            shapes = ((SIZE[left[0]], SIZE[left[1]], 8), (SIZE[left[1]], 8), (8,))
        self.shapes = [(*s, width) for s in shapes]
        self.back = axes[::-1]
        n = SIZE[axes[0]]
        self.far = {1: n // 2 if role == 0 else n // 2 - 1, -1: n // 2 if role == 1 else n // 2 - 1}
        self.ring = [(d, k) for d in (1, -1) for k in range(self.far[d], 0, -1)]
        self.counts = [SIZE[a] - 1 for a in (*axes, *self.back)]
        sums = {d: [d * k for k in range(self.far[d] - 1, 0, -1)] for d in (1, -1)}
        short = -1 if role == 0 else 1
        sums[short] = sums[short] + [0]
        self.own = [sums[-short] + sums[short]] if n == 4 else [sums[1], sums[-1]]

    def offset(self, layer, what, i):
        if what == "rs":
            return sum(self.counts[:i])
        return sum(self.counts[: 3 + i]) + layer * sum(self.counts[3:])

    def scratch(self):
        s = {"own": pltpu.VMEM((len(self.own), *self.shapes[0]), BF16), "acc1": pltpu.VMEM(self.shapes[1], F32)}
        s["acc2"] = pltpu.VMEM((SIZE[self.axes[2]], *self.shapes[2]), F32)
        for i in range(3):
            s[f"recv{i}"] = pltpu.VMEM((self.counts[i], *self.shapes[i]), BF16)
        for i in (1, 2):
            s[f"send{i}"] = pltpu.VMEM((self.counts[i], *self.shapes[i]), BF16)
        if self.kind == "down":
            s["flat"] = pltpu.VMEM(self.shapes[1], F32)
            s["blocks"] = pltpu.VMEM((2, 8, *self.shapes[2]), BF16)
            s["rows"] = pltpu.VMEM((2, *self.shapes[1]), BF16)
        return s

    def chain(self, place, layer, grad, new, out, refs, sems, update):
        send_sem, recv_sem, local_sem, free_sem, place_of = sems
        axes, back, shapes, cols = self.axes, self.back, self.shapes, self.cols
        base, first_local = place_of * MESSAGES, place_of * 6

        def name(*m):
            return (layer, id(self), *m)

        def raw(step):
            c = place.chunk(axes[0], step)
            if self.kind == "down":
                return grad.at[c, :, :, cols] if axes[0] == "x" else grad.at[:, c, :, cols]
            return grad.at[(*(c if a == axes[0] else slice(None) for a in "xyz"), slice(None), cols)]

        def received(d, k):
            return refs["recv0"].at[self.ring.index((d, k))]

        def source(d, k):
            return received(d, k + 1) if k < self.far[d] else raw(d * k)

        def part(i, step):
            c = place.chunk(back[i], step)
            if self.kind == "down" and i == 0:
                return refs["blocks"].at[layer, c]
            known = {a: (slice(None) if a in back[:i] else c if a == back[i] else place.chunk(a, 0)) for a in "xyz"}
            if self.kind == "down":
                return out.at[known["x"], known["y"], :, cols]
            return out.at[known["x"], known["y"], known["z"], :, cols]

        def like(what, i):
            return refs[f"recv{i}"].at[0] if what == "rs" else part(i, 0)

        def send(what, i, n, src, dst, device):
            n = base + self.offset(layer, what, i) + n
            pltpu.make_async_remote_copy(src, dst, send_sem.at[n], recv_sem.at[n], device_id=device, device_id_type=LOGICAL).start()

        def wait(sem, what, i, n):
            ref = like(what, i)
            pltpu.make_async_copy(ref, ref, sem.at[base + self.offset(layer, what, i) + n]).wait()

        def wait_all(sem, what, i):
            count = self.counts[i if what == "rs" else 3 + i]
            lax.fori_loop(0, count, lambda n, c: (wait(sem, what, i, n), c)[1], 0)

        def ring_send(d, k):
            send("rs", 0, self.ring.index((d, k)), source(d, k), received(d, k), place.ring[axes[0], d][1])

        def ring_back(d, k):
            there = part(2, -d * (k - 1))
            send("ag", 2, self.ring.index((d, k)), there, there, place.ring[back[2], d][1])

        def to_each(what, i, f):
            axis = (axes if what == "rs" else back)[i]

            def one(step, c):
                send(what, i, step - 1, *f(step), place.partner(axis, step))
                return c

            lax.fori_loop(1, SIZE[axis], one, 0)

        def own_copy(step):
            b = next(b for b, seq in enumerate(self.own) if step in seq)
            return pltpu.make_async_copy(raw(step), refs["own"].at[b], local_sem.at[first_local + b])

        def own(step):
            b = next(b for b, seq in enumerate(self.own) if step in seq)
            mine = refs["own"].at[b]
            pltpu.make_async_copy(mine, mine, local_sem.at[first_local + b]).wait()
            return mine

        def begin():
            if layer == 0:
                for i in (1, 2):
                    wait_all(send_sem, "rs", i)
                for d in (1, -1):
                    wait(send_sem, "rs", 0, self.ring.index((d, self.far[d])))
                pl.semaphore_wait(free_sem.at[place_of], PARTNERS)
            for d in (1, -1):
                ring_send(d, self.far[d])
            for seq in self.own:
                own_copy(seq[0]).start()

        def add(d, k):
            wait(recv_sem, "rs", 0, self.ring.index((d, k + 1)))
            theirs, mine = received(d, k + 1), own(d * k)

            def f(at):
                theirs[at] = (mine[at].astype(F32) + theirs[at].astype(F32)).astype(BF16)

            each(shapes[0], f)
            for seq in self.own:
                if d * k in seq[:-1]:
                    own_copy(seq[seq.index(d * k) + 1]).start()
            ring_send(d, k)

        def end_0():
            mine = own(0)
            for d in (1, -1):
                wait(recv_sem, "rs", 0, self.ring.index((d, 1)))

            def total(step):
                c = place.chunk(axes[1], step)
                return mine[c].astype(F32) + received(1, 1)[c].astype(F32) + received(-1, 1)[c].astype(F32)

            def f(step):
                to = refs["send1"].at[step - 1]
                to[...] = total(step).astype(BF16)
                return to, refs["recv1"].at[step - 1]

            to_each("rs", 1, f)
            refs["acc1"][...] = total(0)

        def end_1():
            wait_all(recv_sem, "rs", 1)
            acc2 = refs["acc2"]
            total = refs["acc1"][...]
            for n in range(self.counts[1]):
                total = total + refs["recv1"][n].astype(F32)
            if self.kind == "down":
                refs["flat"][...] = total
                for z in range(8):
                    acc2[z, :22, :] = refs["flat"][22 * z : 22 * z + 22, :]
            else:
                acc2[...] = total

            def f(step):
                to = refs["send2"].at[step - 1]
                to[...] = acc2[place.chunk(axes[2], step)].astype(BF16)
                return to, refs["recv2"].at[step - 1]

            to_each("rs", 2, f)

        def end_2():
            wait_all(recv_sem, "rs", 2)
            mine = refs["acc2"][place.chunk(axes[2], 0)]
            update(lax.fori_loop(0, self.counts[2], lambda n, t: t + refs["recv2"][n].astype(F32), mine))
            if layer == 1:
                for d, k in self.ring:
                    if k < self.far[d]:
                        wait(send_sem, "rs", 0, self.ring.index((d, k)))
                place.tell(free_sem.at[place_of])
            mine_copy(0).start()
            to_each("ag", 0, lambda step: (new.at[:, cols], part(0, 0)))

        def mine_copy(i):
            return pltpu.make_async_copy(new.at[:, cols] if i == 0 else refs["rows"].at[layer], part(i, 0), local_sem.at[first_local + 2 + 2 * layer + i])

        def next_back(i):
            wait_all(recv_sem, "ag", i - 1)
            if i == 1:
                mine_copy(0).wait()
            if self.kind == "down":
                if i == 1:
                    for z in range(8):
                        refs["flat"][22 * z : 22 * z + 22, :] = refs["blocks"][layer, z, :22, :].astype(F32)
                    refs["rows"][layer] = refs["flat"][...].astype(BF16)
                    mine_copy(1).start()
                else:
                    mine_copy(1).wait()
            if i == 1:
                to_each("ag", 1, lambda step: (refs["rows"].at[layer] if self.kind == "down" else part(1, 0), part(1, 0)))
            else:
                for d in (1, -1):
                    ring_back(d, 1)

        def forward(d, k):
            wait(recv_sem, "ag", 2, self.ring.index((d, k - 1)))
            ring_back(d, k)

        def finish():
            for d in (1, -1):
                wait(recv_sem, "ag", 2, self.ring.index((d, self.far[d])))
            for i in range(3):
                wait_all(send_sem, "ag", i)
                if layer == 0:
                    wait_all(send_sem, "rs", i)

        def listed(what, i, ms):
            axis = (axes if what == "rs" else back)[i]
            held = 8
            for a in back[:i]:
                held *= SIZE[a]
            nbytes = volume(shapes[i]) if what == "rs" else 2 * self.width * ((24, 176, 704)[i] if self.kind == "down" else held)
            n, found = SIZE[axis], []
            for d, k in ms:
                hops = 1 if d else min(k, n - k)
                way = d or (1 if 2 * k < n or 2 * k == n and self.role == 0 else -1)
                found.append((name(what, i, d, k), (axis, way), nbytes * hops, 0.7 * (hops - 1)))
            return found

        def all_of(what, i):
            return [(0, k) for k in range(1, self.counts[i if what == "rs" else 3 + i] + 1)]

        def names(what, i, ms):
            return [name(what, i, *m) for m in ms]

        far = self.far
        todo = [Action([], begin, listed("rs", 0, [(d, far[d]) for d in (1, -1)]), 0.2)]
        for k in range(max(far.values()) - 1, 0, -1):
            for d in (1, -1):
                if k < far[d]:
                    todo.append(Action([name("rs", 0, d, k + 1)], functools.partial(add, d, k), listed("rs", 0, [(d, k)]), 0.5))
        todo.append(Action(names("rs", 0, [(1, 1), (-1, 1)]), end_0, listed("rs", 1, all_of("rs", 1)), 0.7))
        todo.append(Action(names("rs", 1, all_of("rs", 1)), end_1, listed("rs", 2, all_of("rs", 2)), 0.4))
        todo.append(Action(names("rs", 2, all_of("rs", 2)), end_2, listed("ag", 0, all_of("ag", 0)), 0.6, True))
        todo.append(Action(names("ag", 0, all_of("ag", 0)), functools.partial(next_back, 1), listed("ag", 1, all_of("ag", 1)), 0.3))
        todo.append(Action(names("ag", 1, all_of("ag", 1)), functools.partial(next_back, 2), listed("ag", 2, [(1, 1), (-1, 1)]), 0.2))
        for k in range(2, max(far.values()) + 1):
            for d in (1, -1):
                if k <= far[d]:
                    todo.append(Action([name("ag", 2, d, k - 1)], functools.partial(forward, d, k), listed("ag", 2, [(d, k)]), 0.1))
        todo.append(Action(names("ag", 2, [(d, far[d]) for d in (1, -1)]), finish, [], 0.3))
        return todo


NN = (((1,), (0,)), ((), ()))
NT = (((1,), (1,)), ((), ()))
TN = (((0,), (0,)), ((), ()))
KINDS = ("gate", "up", "down")
ROWS = {"gate": 8, "up": 8, "down": 22}
VIEWS = {"gate": (4, 4, 8, 8, FF), "up": (4, 4, 8, 8, FF), "down": (4, 4, 176, D)}
TILE = 256
TILES = FF // TILE
HALF = T // 2


def dot(a, b, dims=NN):
    return lax.dot_general(a, b, dims, preferred_element_type=F32)


def params(mib=60):
    return pltpu.CompilerParams(vmem_limit_bytes=mib * 1024 * 1024)


def normed(h):
    wide = h.astype(F32)
    return (wide * lax.rsqrt(jnp.mean(wide * wide, -1, keepdims=True) + 1e-6)).astype(BF16)


def gates(x, w_gate, w_up, layer):
    def kernel(x_ref, wg, wu, a_ref, g_ref, u_ref, p_ref):
        @pl.when(pl.program_id(0) == 0)
        def _():
            a_ref[...] = normed(x_ref[...])

        a = a_ref[...]
        g, u = dot(a, wg[0]), dot(a, wu[0])
        g_ref[...], u_ref[...] = g, u
        p_ref[...] = (g * jax.nn.sigmoid(g) * u).astype(BF16)

    whole = pl.BlockSpec((T, D), lambda j: (0, 0))
    w = pl.BlockSpec((1, D, TILE), lambda j: (layer, 0, j))
    o = pl.BlockSpec((T, TILE), lambda j: (0, j))
    shapes = [((T, D), BF16), ((T, FF), F32), ((T, FF), F32), ((T, FF), BF16)]
    return pl.pallas_call(
        kernel,
        grid=(TILES,),
        in_specs=[whole, w, w],
        out_specs=[whole, o, o, o],
        out_shape=[jax.ShapeDtypeStruct(*s) for s in shapes],
        compiler_params=params(),
        name="gates",
    )(x, w_gate, w_up)


def down(p, w_down, h, layer, rows=512):
    def kernel(p_ref, w, h_ref, o_ref, a_ref):
        h1 = h_ref[...] + dot(p_ref[...], w[0]).astype(BF16)
        o_ref[...] = h1
        a_ref[...] = normed(h1)

    def row(n):
        return pl.BlockSpec((rows, n), lambda i: (i, 0))

    return pl.pallas_call(
        kernel,
        grid=(T // rows,),
        in_specs=[row(FF), pl.BlockSpec((1, FF, D), lambda i: (layer, 0, 0), pipeline_mode=pl.Buffered(1)), row(D)],
        out_specs=[row(D), row(D)],
        out_shape=[jax.ShapeDtypeStruct((T, D), BF16)] * 2,
        compiler_params=params(),
        name="down",
    )(p, w_down, h)


def split(g, u, dp):
    s = jax.nn.sigmoid(g)
    silu = g * s
    return silu * u, dp * u * (s + silu * (1 - s)), dp * silu


def tile(j):
    return pl.ds(pl.multiple_of(j * TILE, TILE), TILE)


LAST = (TILES, (4.0, 2.0, 1.3))
STATES = (8, (3.8,))
DOWN0 = (TILES, (1.9,))
FIRST = (TILES, (2.0, 2.3))
PARTS = (LAST, STATES, DOWN0, FIRST)


def tick_list():
    times, starts = [], []
    for n, each_time in PARTS:
        starts.append(len(times))
        times += list(each_time) * n
        times.append(0.5)
    return times, starts


STRIPS = [
    ("gate", 0, 768, 1, "zxy"),
    ("up", 0, 768, 0, "zxy"),
    ("gate", 768, 768, 1, "xyz"),
    ("up", 768, 768, 0, "yxz"),
    ("gate", 1536, 512, 1, "xyz"),
    ("up", 1536, 512, 1, "zxy"),
    ("gate", 2048, 512, 0, "zxy"),
    ("up", 2048, 512, 1, "yxz"),
    ("gate", 2560, 256, 0, "xyz"),
    ("up", 2560, 256, 1, "zxy"),
    ("down", 0, 256, 0, "xyz"),
    ("down", 256, 256, 1, "xyz"),
    ("down", 512, 256, 0, "yxz"),
    ("down", 768, 256, 0, "yxz"),
]


def releases(layer, strip, starts):
    last_tile = (strip.start + strip.width) // TILE - 1
    if layer == 1:
        n = len(LAST[1])
        return starts[0] + (TILES * n if strip.kind == "down" or last_tile == TILES - 1 else last_tile * n + n - 1)
    if strip.kind == "down":
        return starts[2] + TILES * len(DOWN0[1])
    n = len(FIRST[1])
    return starts[3] + (TILES * n if last_tile == TILES - 1 else (last_tile + 1) * n)


def make_strips():
    return [Strip(*s) for s in STRIPS]


def backward(a1, h1, dy, a0, p0, gate0, up0, weights, blocks, m, v):
    strips = make_strips()
    n_messages = MESSAGES * len(strips)
    scratch, names = [], []
    for s in strips:
        for k, shape in s.scratch().items():
            names.append((s, k))
            scratch.append(shape)

    def kernel(*refs):
        a1, h1, dy, a0, p0, gate0, up0, wg, wu, wd = refs[:10]
        old, m, v = (dict(zip(KINDS, refs[10 + 3 * i :])) for i in range(3))
        outs, sums = (dict(zip(KINDS, refs[19 + 3 * i :])) for i in range(2))
        grads = [dict(zip(KINDS, refs[25 + 3 * i :])) for i in range(2)]
        dgate, dup, dh = refs[31:34]
        refs = refs[34:]
        new = dict(zip(KINDS, refs))
        send_sem, recv_sem, local_sem, free_sem = refs[3:7]
        refs = refs[7:]
        place = Place()
        place.greet()
        new["down"][...] = jnp.zeros(new["down"].shape, BF16)
        times, starts = tick_list()
        chains, before = [], {}
        for n, s in enumerate(strips):
            mine = {k: r for (t, k), r in zip(names, refs) if t is s}
            for layer in (1, 0):

                def update(g, s=s, layer=layer):
                    rows = ROWS[s.kind]
                    at = (layer, pl.ds(0, rows), s.cols)
                    g = g[:rows].astype(BF16)
                    sums[s.kind][at] = g
                    g = g.astype(F32)
                    w = old[s.kind][at].astype(F32)
                    m1 = 0.9 * m[s.kind][at] + 0.1 * g
                    v1 = 0.95 * v[s.kind][at] + 0.05 * g * g
                    new[s.kind][at] = (w - 0.02 * (m1 * lax.rsqrt(v1 + 1e-8) + 0.1 * w)).astype(BF16)

                grad = grads[layer][s.kind].reshape(*VIEWS[s.kind])
                sems = (send_sem, recv_sem, local_sem, free_sem, n)
                a = s.chain(place, layer, grad, new[s.kind].at[layer], outs[s.kind].at[layer], mine, sems, update)
                chains.append(Chain(a, releases(layer, s, starts), before.get(s)))
                before[s] = chains[-1]
        placed, rest, _ = plan(chains, times)

        def tick(part, j, i):
            n, each_time = PARTS[part]
            per = len(each_time)
            if j is None:
                for a in placed[starts[part] + n * per]:
                    a.do()
                return
            for when in range(n):
                here = placed[starts[part] + when * per + i]
                if here:

                    @pl.when(j == when)
                    def _(here=here):
                        for a in here:
                            a.do()

        last_part(tick, a1, dy, wg.at[1], wu.at[1], wd.at[1], dgate, dup, grads[1])
        states_part(tick, dgate, dup, wg.at[1], wu.at[1], h1, dy, dh)
        down0_part(tick, p0, dh, grads[0])
        first_part(tick, a0, dh, wd.at[0], gate0, up0, grads[0])
        for a in rest:
            a.do()

    hbm = pl.BlockSpec(memory_space=pl.ANY)
    vmem = pl.BlockSpec(memory_space=pltpu.VMEM)
    wide = [jax.ShapeDtypeStruct((2, *VIEWS[k]), BF16) for k in KINDS]
    own = [jax.ShapeDtypeStruct((2, ROWS[k], VIEWS[k][-1]), BF16) for k in KINDS]
    local = [jax.ShapeDtypeStruct((FF, D) if k == "down" else (D, FF), BF16) for _ in range(2) for k in KINDS]
    local += [jax.ShapeDtypeStruct((T, FF), BF16)] * 2 + [jax.ShapeDtypeStruct((T, D), BF16)]
    out = pl.pallas_call(
        kernel,
        out_shape=wide + own + local,
        in_specs=[hbm] * 10 + [vmem] * 9,
        out_specs=[hbm] * 3 + [vmem] * 3 + [hbm] * 9,
        scratch_shapes=[pltpu.VMEM((2, -(-ROWS[k] // 8) * 8, VIEWS[k][-1]), BF16) for k in KINDS]
        + [pltpu.SemaphoreType.DMA((n_messages,))] * 2
        + [pltpu.SemaphoreType.DMA((6 * len(strips),)), pltpu.SemaphoreType.REGULAR((len(strips),))]
        + scratch,
        compiler_params=pltpu.CompilerParams(collective_id=1, has_side_effects=True, vmem_limit_bytes=67043328),
        name="backward",
    )(a1, h1, dy, a0, p0, gate0, up0, *weights, *blocks, *m, *v)
    return out[:3], out[3:6]


def last_part(tick, a1, dy, wg, wu, wd, dgate, dup, grads):
    def body(a, y, g_tile, u_tile, d_tile, p, dgu, og, ou, od, sem, in_sem, out_sem):
        dg, du = dgu.at[:, pl.ds(0, TILE)], dgu.at[:, pl.ds(TILE, TILE)]

        first = [pltpu.make_async_copy(s, d, sem.at[i]) for i, (s, d) in enumerate(((a1, a), (dy, y)))]

        def ins(j):
            s = lax.rem(j, 2)
            pairs = ((wg.at[:, tile(j)], g_tile.at[s]), (wu.at[:, tile(j)], u_tile.at[s]), (wd.at[tile(j)], d_tile.at[s]))
            return [pltpu.make_async_copy(src, dst, in_sem.at[s, i]) for i, (src, dst) in enumerate(pairs)]

        def outs(j):
            pairs = ((og, grads["gate"].at[:, tile(j)]), (ou, grads["up"].at[:, tile(j)]), (od, grads["down"].at[tile(j)]))
            pairs += ((dg, dgate.at[:, tile(j)]), (du, dup.at[:, tile(j)]))
            return [pltpu.make_async_copy(src, dst, out_sem.at[i]) for i, (src, dst) in enumerate(pairs)]

        for c in first + ins(jnp.int32(0)):
            c.start()
        for c in first:
            c.wait()

        def go(j, carry):
            s = lax.rem(j, 2)
            for c in ins(j):
                c.wait()

            @pl.when(j < TILES - 1)
            def _():
                for c in ins(j + 1):
                    c.start()

            for half in range(2):
                rows = pl.ds(half * HALF, HALF)
                g, u = dot(a[rows, :], g_tile[s]), dot(a[rows, :], u_tile[s])
                dp = dot(y[rows, :], d_tile[s], NT).astype(BF16).astype(F32)
                p_, dg_, du_ = split(g, u, dp)
                p[rows, :], dgu[rows, :TILE], dgu[rows, TILE:] = p_.astype(BF16), dg_.astype(BF16), du_.astype(BF16)
            o = outs(j)
            o[3].start()
            o[4].start()
            tick(0, j, 0)
            both = dot(a[...], dgu[...], TN).astype(BF16)
            og[...], ou[...] = both[:, :TILE], both[:, TILE:]
            o[0].start()
            o[1].start()
            tick(0, j, 1)

            @pl.when(j > 0)
            def _():
                outs(j - 1)[2].wait()

            od[...] = dot(p[...], y[...], TN).astype(BF16)
            o[2].start()
            for i in (3, 4, 0, 1):
                o[i].wait()
            tick(0, j, 2)
            return carry

        lax.fori_loop(0, TILES, go, 0)
        outs(jnp.int32(TILES - 1))[2].wait()
        tick(0, None, 0)

    tiles = [pltpu.VMEM((2, D, TILE), BF16)] * 2 + [pltpu.VMEM((2, TILE, D), BF16)]
    pl.run_scoped(
        body,
        *[pltpu.VMEM((T, D), BF16)] * 2,
        *tiles,
        pltpu.VMEM((T, TILE), BF16),
        pltpu.VMEM((T, 2 * TILE), BF16),
        *[pltpu.VMEM((D, TILE), BF16)] * 2,
        pltpu.VMEM((TILE, D), BF16),
        pltpu.SemaphoreType.DMA((2,)),
        pltpu.SemaphoreType.DMA((2, 3)),
        pltpu.SemaphoreType.DMA((5,)),
    )


def states_part(tick, dgate, dup, wg, wu, h1, dy, dh, rows=256):
    n = T // rows

    def body(wg_all, wu_all, dg, du, h, y, o, sem, in_sem, out_sem):
        first = [pltpu.make_async_copy(s, d, sem.at[i]) for i, (s, d) in enumerate(((wg, wg_all), (wu, wu_all)))]

        def at(j):
            return pl.ds(pl.multiple_of(j * rows, rows), rows)

        def ins(j):
            s = lax.rem(j, 2)
            pairs = ((dgate, dg), (dup, du), (h1, h), (dy, y))
            return [pltpu.make_async_copy(src.at[at(j)], dst.at[s], in_sem.at[s, i]) for i, (src, dst) in enumerate(pairs)]

        def out(j):
            return pltpu.make_async_copy(o, dh.at[at(j)], out_sem)

        for c in first + ins(jnp.int32(0)):
            c.start()
        for c in first:
            c.wait()

        def go(j, carry):
            s = lax.rem(j, 2)
            for c in ins(j):
                c.wait()

            @pl.when(j < n - 1)
            def _():
                for c in ins(j + 1):
                    c.start()

            da = (dot(dg[s], wg_all[...], NT) + dot(du[s], wu_all[...], NT)).astype(BF16).astype(F32)
            wide = h[s].astype(F32)
            scale = lax.rsqrt(jnp.mean(wide * wide, -1, keepdims=True) + 1e-6)
            inner = jnp.mean(da * wide, -1, keepdims=True)
            back = da * scale - wide * (scale * scale * scale * inner)

            @pl.when(j > 0)
            def _():
                out(j - 1).wait()

            o[...] = (y[s].astype(F32) + back).astype(BF16)
            out(j).start()
            tick(1, j, 0)
            return carry

        lax.fori_loop(0, n, go, 0)
        out(jnp.int32(n - 1)).wait()
        tick(1, None, 0)

    pl.run_scoped(
        body,
        *[pltpu.VMEM((D, FF), BF16)] * 2,
        *[pltpu.VMEM((2, rows, FF), BF16)] * 2,
        *[pltpu.VMEM((2, rows, D), BF16)] * 2,
        pltpu.VMEM((rows, D), BF16),
        pltpu.SemaphoreType.DMA((2,)),
        pltpu.SemaphoreType.DMA((2, 4)),
        pltpu.SemaphoreType.DMA,
    )


def down0_part(tick, p0, dh, grads):
    def body(y, p, od, sem, in_sem, out_sem):
        first = pltpu.make_async_copy(dh, y, sem)

        def load(j):
            s = lax.rem(j, 2)
            return pltpu.make_async_copy(p0.at[:, tile(j)], p.at[s], in_sem.at[s])

        def out(j):
            return pltpu.make_async_copy(od, grads["down"].at[tile(j)], out_sem)

        first.start()
        load(jnp.int32(0)).start()
        first.wait()

        def go(j, carry):
            s = lax.rem(j, 2)
            load(j).wait()

            @pl.when(j < TILES - 1)
            def _():
                load(j + 1).start()

            @pl.when(j > 0)
            def _():
                out(j - 1).wait()

            od[...] = dot(p[s], y[...], TN).astype(BF16)
            out(j).start()
            tick(2, j, 0)
            return carry

        lax.fori_loop(0, TILES, go, 0)
        out(jnp.int32(TILES - 1)).wait()
        tick(2, None, 0)

    pl.run_scoped(
        body,
        pltpu.VMEM((T, D), BF16),
        pltpu.VMEM((2, T, TILE), BF16),
        pltpu.VMEM((TILE, D), BF16),
        pltpu.SemaphoreType.DMA,
        pltpu.SemaphoreType.DMA((2,)),
        pltpu.SemaphoreType.DMA,
    )


def first_part(tick, a0, dh, wd, gate0, up0, grads):
    def body(a, y, d_tile, g, u, dgu, og, ou, sem, in_sem, out_sem):
        first = [pltpu.make_async_copy(s, d, sem.at[i]) for i, (s, d) in enumerate(((a0, a), (dh, y)))]

        def ins(j):
            s = lax.rem(j, 2)
            pairs = ((wd.at[tile(j)], d_tile.at[s]), (gate0.at[:, tile(j)], g.at[s]), (up0.at[:, tile(j)], u.at[s]))
            return [pltpu.make_async_copy(src, dst, in_sem.at[s, i]) for i, (src, dst) in enumerate(pairs)]

        def outs(j):
            pairs = ((og, grads["gate"].at[:, tile(j)]), (ou, grads["up"].at[:, tile(j)]))
            return [pltpu.make_async_copy(src, dst, out_sem.at[i]) for i, (src, dst) in enumerate(pairs)]

        for c in first + ins(jnp.int32(0)):
            c.start()
        for c in first:
            c.wait()

        def go(j, carry):
            s = lax.rem(j, 2)
            for c in ins(j):
                c.wait()

            @pl.when(j < TILES - 1)
            def _():
                for c in ins(j + 1):
                    c.start()

            for half in range(2):
                rows = pl.ds(half * HALF, HALF)
                dp = dot(y[rows, :], d_tile[s], NT).astype(BF16).astype(F32)
                _, dg_, du_ = split(g[s, rows, :], u[s, rows, :], dp)
                dgu[rows, :TILE], dgu[rows, TILE:] = dg_.astype(BF16), du_.astype(BF16)

            @pl.when(j > 0)
            def _():
                for c in outs(j - 1):
                    c.wait()

            tick(3, j, 0)
            both = dot(a[...], dgu[...], TN).astype(BF16)
            og[...], ou[...] = both[:, :TILE], both[:, TILE:]
            for c in outs(j):
                c.start()
            tick(3, j, 1)
            return carry

        lax.fori_loop(0, TILES, go, 0)
        for c in outs(jnp.int32(TILES - 1)):
            c.wait()
        tick(3, None, 0)

    pl.run_scoped(
        body,
        *[pltpu.VMEM((T, D), BF16)] * 2,
        pltpu.VMEM((2, TILE, D), BF16),
        *[pltpu.VMEM((2, T, TILE), F32)] * 2,
        pltpu.VMEM((T, 2 * TILE), BF16),
        *[pltpu.VMEM((D, TILE), BF16)] * 2,
        pltpu.SemaphoreType.DMA((2,)),
        pltpu.SemaphoreType.DMA((2, 3)),
        pltpu.SemaphoreType.DMA((2,)),
    )


def moments(sums, m, v):
    def kernel(*refs):
        for g, m_ref, v_ref, new_m, new_v in zip(*(refs[3 * i :][:3] for i in range(5))):
            grad = g[...].astype(F32)
            new_m[...] = 0.9 * m_ref[...] + 0.1 * grad
            new_v[...] = 0.95 * v_ref[...] + 0.05 * grad * grad

    shapes = [jax.ShapeDtypeStruct(t.shape, F32) for t in (*m, *v)]
    out = pl.pallas_call(kernel, out_shape=shapes, name="moments")(*sums, *m, *v)
    return out[:3], out[3:]


def step(x, dy, *arrays):
    weights, m, v = (arrays[i : i + 3] for i in (0, 3, 6))
    w_gate, w_up, w_down = weights
    x, dy = x[0], dy[0]
    me = lax.axis_index("dp")
    blocks = [lax.dynamic_slice_in_dim(w, me * ROWS[k], ROWS[k], 1) for k, w in zip(KINDS, weights)]
    a0, gate0, up0, p0 = gates(x, w_gate, w_up, 0)
    h1, a1 = down(p0, w_down, x, 0)
    whole, sums = backward(a1, h1, dy, a0, p0, gate0, up0, weights, blocks, m, v)
    new_m, new_v = moments(sums, m, v)
    return (*(t.reshape(2, -1, t.shape[-1]) for t in whole), *new_m, *new_v)


def solution(mesh):
    P = jax.sharding.PartitionSpec
    data, state = P(("rep", "dp")), P(None, "dp")
    return jax.shard_map(
        step,
        mesh=mesh,
        in_specs=(data, data, P(), P(), P(), *[state] * 6),
        out_specs=(*[P("rep")] * 3, *[P("rep", "dp")] * 6),
        check_vma=False,
    )
```

time: 3510 us -> 484 us (0.14)
  waiting for transfers between devices: 2560 us -> 0 us
  Pallas kernels: 0 us -> 443 us
  blocking collectives: 435 us -> 0 us
  matrix products: 304 us -> 0 us
  starting transfers between devices: 78.2 us -> 0 us
  other arithmetic: 56.5 us -> 0.01 us
    unnamed x33 -> x0, waiting for transfers between devices: 2080 us -> none
    reshape x3 -> x0, waiting for transfers between devices: 481 us -> none  [step(): t.reshape(-1, *t.shape[2:])]
    pallas_call x0 -> x4, Pallas kernels: none -> 443 us  [the longest x1 389 us: backward(): pl.pallas_call(kernel, out_shape=wide + own + local, in_specs=[hbm] * 10...]
    unnamed x1 -> x0, blocking collectives: 435 us -> none
    dot_general x15 -> x0, matrix products: 304 us -> none  [the longest x5 104 us: layer(): up = jnp.dot(a, w['w_up'], preferred_element_type=jnp.float32)]
    unnamed x26 -> x0, starting transfers between devices: 78 us -> none
    unnamed x5 -> x1, other arithmetic: 45.2 us -> 0.01 us
  transfers between devices with their start and end apart: 29 -> 0, of which waited for: 6 -> 0; matrix products, arithmetic and copies ran while one was open for 19% -> 0% of each run, Pallas kernels for 0% -> 0%
where the time goes in v1:
time: 484 us; the launch traced here: 478 us
  Pallas kernels  443 us (92%)
  local copies, waits for them, and re-layouts  34 us (7%)
    pallas_call x1, Pallas kernels, backward(): pl.pallas_call(kernel, out_shape=wide + own + local, in_specs=[hbm] * 10...  389 us
    pallas_call x1, Pallas kernels, gates(): pl.pallas_call(kernel, grid=(TILES,), in_specs=[whole, w, w], out_specs=[...  32.9 us
    unnamed x15, local copies, waits for them, and re-layouts  30.8 us
    pallas_call x1, Pallas kernels, down(): pl.pallas_call(kernel, grid=(T // rows,), in_specs=[row(FF), pl.BlockSpec...  19.2 us

profile of v1, /device:TPU:1, one launch (start us, length us, event | category | flops | bytes accessed | tf_op | source)
XLA Modules:
  0.0 477.8 jit_solution(1396087688884685159)
XLA Ops:
  0.6 1.6 constant_dynamic-slice_fusion.refs_12_
  2.2 1.6 constant_dynamic-slice_fusion.1
  3.8 1.7 copy.20.refs_15_.refs_5_
  5.5 1.7 copy.21.refs_18_.refs_8_
  7.2 32.9 %gates.1 = (bf16[2048,1024]{1,0:T(8,128)(2,1)}, f32[2048,2816]{1,0:T(8,128)}, f32[2048,2816]{1,0:T(8,128)}, bf16[2048,2816]{1,0:T(8,128)(2,1)}) custom-call(bf16[2048,1024]{1,0:T(8,128)(2,1)} %bitcast.5, bf16[2,1024,2816]{2,1,0:T(8,128)(2,1)} %refs_7_.2, bf16[2,1024,2816]{2,1,0:T(8,128)(2,1)} %refs_8_.2), custom_call_target="tpu_custom_call" | custom-call | tf_op jit(solution)/shard_map/gates/pallas_call | solution.py:415
  40.1 19.2 %down.1 = (bf16[2048,1024]{1,0:T(8,128)(2,1)}, bf16[2048,1024]{1,0:T(8,128)(2,1)}) custom-call(bf16[2048,2816]{1,0:T(8,128)(2,1)} %get-tuple-element.27.p_ref.refs_4_, bf16[2,2816,1024]{2,1,0:T(8,128)(2,1)} %refs_9_.1, bf16[2048,1024]{1,0:T(8,128)(2,1)} %bitcast.6), custom_call_target="tpu_custom_call" | custom-call | tf_op jit(solution)/shard_map/down/pallas_call | solution.py:435
  59.3 388.5 %backward.1 = (bf16[2,4,4,8,8,2816]{5,4,3,2,1,0:T(8,128)(2,1)}, bf16[2,4,4,8,8,2816]{5,4,3,2,1,0:T(8,128)(2,1)}, bf16[2,4,4,176,1024]{4,3,2,1,0:T(8,128)(2,1)}, ...) custom-call(bf16[2048,1024]{1,0:T(8,128)(2,1)} %get-tuple-element.28, ...), custom_call_target="tpu_custom_call" | custom-call | tf_op jit(solution)/shard_map/backward/pallas_call | solution.py:580
  447.8 2.5 moments.1
  450.3 1.7 copy.24
  452.1 1.7 copy.25
  453.8 0.0 copy-start
  453.8 0.0 slice-start
  453.8 0.0 slice-start.1
  453.8 11.7 %copy.29 = bf16[2,1024,2816]{2,1,0:T(8,128)(2,1)} copy(bf16[2,1024,2816]{2,1,0:T(8,128)(2,1)} %bitcast.11) | data formatting | bytes 23068672
  465.5 0.0 copy-done
  465.5 0.0 slice-start.2
  465.5 5.8 %copy.30 = bf16[2,1024,2816]{2,1,0:T(8,128)(2,1)} copy(bf16[2,1024,2816]{2,1,0:T(8,128)(2,1)S(1)} %bitcast.10) | data formatting | bytes 23068672
  471.3 0.0 slice-done
  471.3 0.8 slice-done.1
  472.1 1.2 slice-done.2
  473.3 4.4 copy.31
  (1 shorter events, 0.0 us)
Async XLA Ops:
  453.8 11.7 %copy-start = (bf16[2,4,4,8,8,2816]{5,4,3,2,1,0:T(8,128)(2,1)S(1)}, bf16[2,4,4,8,8,2816]{5,4,3,2,1,0:T(8,128)(2,1)}, u32[]{:S(2)}) copy-start(bf16[2,4,4,8,8,2816]{5,4,3,2,1,0:T(8,128)(2,1)} %get-tuple-element.34) | copy-start | bytes 34603012
  453.8 17.5 %slice-start = ((s8[11534336]{0:T(1024)(128)(4,1)}), s8[4194304]{0:T(1024)(128)(4,1)S(1)}, s32[]{:S(2)}) async-start(s8[11534336]{0:T(1024)(128)(4,1)} %bitcast.7), calls=%async_computation | async-start | bytes 8388608
  453.8 18.3 %slice-start.1 = ((s8[11534336]{0:T(1024)(128)(4,1)}), s8[4194304]{0:T(1024)(128)(4,1)S(1)}, s32[]{:S(2)}) async-start(s8[11534336]{0:T(1024)(128)(4,1)} %bitcast.7), calls=%async_computation.1 | async-start | bytes 8388608
  465.5 7.9 %slice-start.2 = ((s8[11534336]{0:T(1024)(128)(4,1)}), s8[3145728]{0:T(1024)(128)(4,1)S(1)}, s32[]{:S(2)}) async-start(s8[11534336]{0:T(1024)(128)(4,1)} %bitcast.7), calls=%async_computation.2 | async-start | bytes 6291456

commit v2 on v1

--- a/solution.py
+++ b/solution.py
@@ -17,7 +17,7 @@
 
 class Place:
     def __init__(self):
-        me = lax.axis_index("dp")
+        me = self.me = lax.axis_index("dp")
         self.at = {"x": me // 32, "y": (me // 8) % 4, "z": me % 8}
         self.number = lax.axis_index("rep") * 128 + me
         self.ring = {(axis, step): (self.at_step(axis, step), self.partner(axis, step)) for axis in "xyz" for step in (1, -1)}
@@ -59,10 +59,13 @@
         return self.done == len(self.actions)
 
 
-RATE = 46.0e3
-
-
-def plan(chains, ticks, latency=3.0):
+RATE = 45.5e3
+
+
+LATENCY = 3.0
+
+
+def plan(chains, ticks, latency=LATENCY):
     free, arrive, now, placed, rest = {}, {}, 0.0, [], []
 
     def run(c, a, at):
@@ -95,7 +98,7 @@
             here.append(a)
         placed.append(here)
     while not all(c.ended() for c in chains):
-        r, i = min((max(r, now - 1e3), i) for i, c in enumerate(chains) if (r := ready(c, len(ticks))) is not None)
+        r, i = min((max(r, now), i) for i, c in enumerate(chains) if (r := ready(c, len(ticks))) is not None)
         c = chains[i]
         a = c.actions[c.done]
         c.done += 1
@@ -355,21 +358,21 @@
             return [name(what, i, *m) for m in ms]
 
         far = self.far
-        todo = [Action([], begin, listed("rs", 0, [(d, far[d]) for d in (1, -1)]), 0.2)]
+        todo = [Action([], begin, listed("rs", 0, [(d, far[d]) for d in (1, -1)]), 0.06)]
         for k in range(max(far.values()) - 1, 0, -1):
             for d in (1, -1):
                 if k < far[d]:
-                    todo.append(Action([name("rs", 0, d, k + 1)], functools.partial(add, d, k), listed("rs", 0, [(d, k)]), 0.5))
-        todo.append(Action(names("rs", 0, [(1, 1), (-1, 1)]), end_0, listed("rs", 1, all_of("rs", 1)), 0.7))
-        todo.append(Action(names("rs", 1, all_of("rs", 1)), end_1, listed("rs", 2, all_of("rs", 2)), 0.4))
-        todo.append(Action(names("rs", 2, all_of("rs", 2)), end_2, listed("ag", 0, all_of("ag", 0)), 0.6, True))
-        todo.append(Action(names("ag", 0, all_of("ag", 0)), functools.partial(next_back, 1), listed("ag", 1, all_of("ag", 1)), 0.3))
-        todo.append(Action(names("ag", 1, all_of("ag", 1)), functools.partial(next_back, 2), listed("ag", 2, [(1, 1), (-1, 1)]), 0.2))
+                    todo.append(Action([name("rs", 0, d, k + 1)], functools.partial(add, d, k), listed("rs", 0, [(d, k)]), 0.3 if SIZE[axes[0]] == 4 else 0.13))
+        todo.append(Action(names("rs", 0, [(1, 1), (-1, 1)]), end_0, listed("rs", 1, all_of("rs", 1)), 0.4))
+        todo.append(Action(names("rs", 1, all_of("rs", 1)), end_1, listed("rs", 2, all_of("rs", 2)), 0.35))
+        todo.append(Action(names("rs", 2, all_of("rs", 2)), end_2, listed("ag", 0, all_of("ag", 0)), 0.5, True))
+        todo.append(Action(names("ag", 0, all_of("ag", 0)), functools.partial(next_back, 1), listed("ag", 1, all_of("ag", 1)), 0.25))
+        todo.append(Action(names("ag", 1, all_of("ag", 1)), functools.partial(next_back, 2), listed("ag", 2, [(1, 1), (-1, 1)]), 0.15))
         for k in range(2, max(far.values()) + 1):
             for d in (1, -1):
                 if k <= far[d]:
                     todo.append(Action([name("ag", 2, d, k - 1)], functools.partial(forward, d, k), listed("ag", 2, [(d, k)]), 0.1))
-        todo.append(Action(names("ag", 2, [(d, far[d]) for d in (1, -1)]), finish, [], 0.3))
+        todo.append(Action(names("ag", 2, [(d, far[d]) for d in (1, -1)]), finish, [], 0.15))
         return todo
 
 
@@ -388,59 +391,9 @@
     return lax.dot_general(a, b, dims, preferred_element_type=F32)
 
 
-def params(mib=60):
-    return pltpu.CompilerParams(vmem_limit_bytes=mib * 1024 * 1024)
-
-
 def normed(h):
     wide = h.astype(F32)
     return (wide * lax.rsqrt(jnp.mean(wide * wide, -1, keepdims=True) + 1e-6)).astype(BF16)
-
-
-def gates(x, w_gate, w_up, layer):
-    def kernel(x_ref, wg, wu, a_ref, g_ref, u_ref, p_ref):
-        @pl.when(pl.program_id(0) == 0)
-        def _():
-            a_ref[...] = normed(x_ref[...])
-
-        a = a_ref[...]
-        g, u = dot(a, wg[0]), dot(a, wu[0])
-        g_ref[...], u_ref[...] = g, u
-        p_ref[...] = (g * jax.nn.sigmoid(g) * u).astype(BF16)
-
-    whole = pl.BlockSpec((T, D), lambda j: (0, 0))
-    w = pl.BlockSpec((1, D, TILE), lambda j: (layer, 0, j))
-    o = pl.BlockSpec((T, TILE), lambda j: (0, j))
-    shapes = [((T, D), BF16), ((T, FF), F32), ((T, FF), F32), ((T, FF), BF16)]
-    return pl.pallas_call(
-        kernel,
-        grid=(TILES,),
-        in_specs=[whole, w, w],
-        out_specs=[whole, o, o, o],
-        out_shape=[jax.ShapeDtypeStruct(*s) for s in shapes],
-        compiler_params=params(),
-        name="gates",
-    )(x, w_gate, w_up)
-
-
-def down(p, w_down, h, layer, rows=512):
-    def kernel(p_ref, w, h_ref, o_ref, a_ref):
-        h1 = h_ref[...] + dot(p_ref[...], w[0]).astype(BF16)
-        o_ref[...] = h1
-        a_ref[...] = normed(h1)
-
-    def row(n):
-        return pl.BlockSpec((rows, n), lambda i: (i, 0))
-
-    return pl.pallas_call(
-        kernel,
-        grid=(T // rows,),
-        in_specs=[row(FF), pl.BlockSpec((1, FF, D), lambda i: (layer, 0, 0), pipeline_mode=pl.Buffered(1)), row(D)],
-        out_specs=[row(D), row(D)],
-        out_shape=[jax.ShapeDtypeStruct((T, D), BF16)] * 2,
-        compiler_params=params(),
-        name="down",
-    )(p, w_down, h)
 
 
 def split(g, u, dp):
@@ -453,10 +406,10 @@
     return pl.ds(pl.multiple_of(j * TILE, TILE), TILE)
 
 
-LAST = (TILES, (4.0, 2.0, 1.3))
-STATES = (8, (3.8,))
-DOWN0 = (TILES, (1.9,))
-FIRST = (TILES, (2.0, 2.3))
+LAST = (TILES, (4.1, 2.05, 1.4))
+STATES = (8, (4.3,))
+DOWN0 = (TILES, (1.76,))
+FIRST = (TILES, (2.24, 2.4))
 PARTS = (LAST, STATES, DOWN0, FIRST)
 
 
@@ -472,18 +425,18 @@
 STRIPS = [
     ("gate", 0, 768, 1, "zxy"),
     ("up", 0, 768, 0, "zxy"),
-    ("gate", 768, 768, 1, "xyz"),
+    ("gate", 768, 768, 0, "xyz"),
     ("up", 768, 768, 0, "yxz"),
     ("gate", 1536, 512, 1, "xyz"),
-    ("up", 1536, 512, 1, "zxy"),
-    ("gate", 2048, 512, 0, "zxy"),
-    ("up", 2048, 512, 1, "yxz"),
-    ("gate", 2560, 256, 0, "xyz"),
+    ("up", 1536, 512, 0, "yxz"),
+    ("gate", 2048, 512, 1, "zxy"),
+    ("up", 2048, 512, 0, "yxz"),
+    ("gate", 2560, 256, 0, "zxy"),
     ("up", 2560, 256, 1, "zxy"),
-    ("down", 0, 256, 0, "xyz"),
-    ("down", 256, 256, 1, "xyz"),
-    ("down", 512, 256, 0, "yxz"),
-    ("down", 768, 256, 0, "yxz"),
+    ("down", 0, 256, 1, "yxz"),
+    ("down", 256, 256, 1, "yxz"),
+    ("down", 512, 256, 1, "xyz"),
+    ("down", 768, 256, 0, "xyz"),
 ]
 
 
@@ -502,7 +455,7 @@
     return [Strip(*s) for s in STRIPS]
 
 
-def backward(a1, h1, dy, a0, p0, gate0, up0, weights, blocks, m, v):
+def train(x, dy, weights, block, m, v):
     strips = make_strips()
     n_messages = MESSAGES * len(strips)
     scratch, names = [], []
@@ -512,17 +465,25 @@
             scratch.append(shape)
 
     def kernel(*refs):
-        a1, h1, dy, a0, p0, gate0, up0, wg, wu, wd = refs[:10]
-        old, m, v = (dict(zip(KINDS, refs[10 + 3 * i :])) for i in range(3))
-        outs, sums = (dict(zip(KINDS, refs[19 + 3 * i :])) for i in range(2))
-        grads = [dict(zip(KINDS, refs[25 + 3 * i :])) for i in range(2)]
-        dgate, dup, dh = refs[31:34]
-        refs = refs[34:]
+        x, dy, wg, wu, wd = refs[:5]
+        m, v = (dict(zip(KINDS, refs[6 + 3 * i :])) for i in range(2))
+        outs, sums = (dict(zip(KINDS, refs[12 + 3 * i :])) for i in range(2))
+        grads = [dict(zip(KINDS, refs[18 + 3 * i :])) for i in range(2)]
+        dgate, dup, p0, gate0, up0, a0, h1 = refs[24:31]
+        old = {"gate": refs[31], "up": refs[32], "down": refs[5]}
+        refs = refs[33:]
         new = dict(zip(KINDS, refs))
-        send_sem, recv_sem, local_sem, free_sem = refs[3:7]
-        refs = refs[7:]
+        send_sem, recv_sem, local_sem, free_sem, old_sem = refs[3:8]
+        refs = refs[8:]
         place = Place()
-        place.greet()
+        mine = pl.ds(pl.multiple_of(place.me * 8, 8), 8)
+        loads = [pltpu.make_async_copy(w.at[:, mine], old[k], old_sem.at[i]) for i, (k, w) in enumerate((("gate", wg), ("up", wu)))]
+        for c in loads:
+            c.start()
+        barrier = pltpu.get_barrier_semaphore()
+        place.tell(barrier)
+        for c in loads:
+            c.wait()
         new["down"][...] = jnp.zeros(new["down"].shape, BF16)
         times, starts = tick_list()
         chains, before = [], {}
@@ -537,8 +498,9 @@
                     sums[s.kind][at] = g
                     g = g.astype(F32)
                     w = old[s.kind][at].astype(F32)
-                    m1 = 0.9 * m[s.kind][at] + 0.1 * g
-                    v1 = 0.95 * v[s.kind][at] + 0.05 * g * g
+                    moments_at = (at[1], layer, s.cols) if s.kind == "down" else at
+                    m1 = 0.9 * m[s.kind][moments_at] + 0.1 * g
+                    v1 = 0.95 * v[s.kind][moments_at] + 0.05 * g * g
                     new[s.kind][at] = (w - 0.02 * (m1 * lax.rsqrt(v1 + 1e-8) + 0.1 * w)).astype(BF16)
 
                 grad = grads[layer][s.kind].reshape(*VIEWS[s.kind])
@@ -564,10 +526,21 @@
                         for a in here:
                             a.do()
 
-        last_part(tick, a1, dy, wg.at[1], wu.at[1], wd.at[1], dgate, dup, grads[1])
-        states_part(tick, dgate, dup, wg.at[1], wu.at[1], h1, dy, dh)
-        down0_part(tick, p0, dh, grads[0])
-        first_part(tick, a0, dh, wd.at[0], gate0, up0, grads[0])
+        def parts(a, y, sem):
+            load = pltpu.make_async_copy(dy, y, sem)
+            load.start()
+            forward_part(x, wg.at[0], wu.at[0], wd.at[0], a0, gate0, up0, p0, h1, a)
+            load.wait()
+            pl.semaphore_wait(barrier, PARTNERS)
+            last_part(tick, a, y, wg.at[1], wu.at[1], wd.at[1], dgate, dup, grads[1])
+            states_part(tick, dgate, dup, wg.at[1], wu.at[1], h1, y, a)
+            load = pltpu.make_async_copy(a0, a, sem)
+            load.start()
+            down0_part(tick, p0, y, grads[0])
+            load.wait()
+            first_part(tick, a, y, wd.at[0], gate0, up0, grads[0])
+
+        pl.run_scoped(parts, *[pltpu.VMEM((T, D), BF16)] * 2, pltpu.SemaphoreType.DMA)
         for a in rest:
             a.do()
 
@@ -576,27 +549,146 @@
     wide = [jax.ShapeDtypeStruct((2, *VIEWS[k]), BF16) for k in KINDS]
     own = [jax.ShapeDtypeStruct((2, ROWS[k], VIEWS[k][-1]), BF16) for k in KINDS]
     local = [jax.ShapeDtypeStruct((FF, D) if k == "down" else (D, FF), BF16) for _ in range(2) for k in KINDS]
-    local += [jax.ShapeDtypeStruct((T, FF), BF16)] * 2 + [jax.ShapeDtypeStruct((T, D), BF16)]
+    local += [jax.ShapeDtypeStruct((T, FF), t) for t in (BF16, BF16, BF16, F32, F32)] + [jax.ShapeDtypeStruct((T, D), BF16)] * 2
     out = pl.pallas_call(
         kernel,
         out_shape=wide + own + local,
-        in_specs=[hbm] * 10 + [vmem] * 9,
-        out_specs=[hbm] * 3 + [vmem] * 3 + [hbm] * 9,
-        scratch_shapes=[pltpu.VMEM((2, -(-ROWS[k] // 8) * 8, VIEWS[k][-1]), BF16) for k in KINDS]
+        in_specs=[hbm] * 5 + [vmem] * 7,
+        out_specs=[hbm] * 3 + [vmem] * 3 + [hbm] * 13,
+        scratch_shapes=[pltpu.VMEM((2, 8, FF), BF16)] * 2
+        + [pltpu.VMEM((2, -(-ROWS[k] // 8) * 8, VIEWS[k][-1]), BF16) for k in KINDS]
         + [pltpu.SemaphoreType.DMA((n_messages,))] * 2
-        + [pltpu.SemaphoreType.DMA((6 * len(strips),)), pltpu.SemaphoreType.REGULAR((len(strips),))]
+        + [pltpu.SemaphoreType.DMA((6 * len(strips),)), pltpu.SemaphoreType.REGULAR((len(strips),)), pltpu.SemaphoreType.DMA((2,))]
         + scratch,
         compiler_params=pltpu.CompilerParams(collective_id=1, has_side_effects=True, vmem_limit_bytes=67043328),
-        name="backward",
-    )(a1, h1, dy, a0, p0, gate0, up0, *weights, *blocks, *m, *v)
+        name="train",
+    )(x, dy, *weights, block, *m, *v)
     return out[:3], out[3:6]
 
 
-def last_part(tick, a1, dy, wg, wu, wd, dgate, dup, grads):
-    def body(a, y, g_tile, u_tile, d_tile, p, dgu, og, ou, od, sem, in_sem, out_sem):
+def forward_part(x, wg, wu, wd, a0, gate0, up0, p0, h1, a):
+    rows, tall = 256, 512
+    n, n_tall = T // rows, T // tall
+
+    def at(j, rows=rows):
+        return pl.ds(pl.multiple_of(j * rows, rows), rows)
+
+    def body(g_tile, u_tile, in_sem, a_sem):
+        store_a = pltpu.make_async_copy(a, a0, a_sem)
+
+        def ins(j):
+            s = lax.rem(j, 2)
+            pairs = ((wg, g_tile), (wu, u_tile))
+            return [pltpu.make_async_copy(src.at[:, tile(j)], dst.at[s], in_sem.at[s, i]) for i, (src, dst) in enumerate(pairs)]
+
+        def norm(h, sem):
+            def load(j):
+                return pltpu.make_async_copy(x.at[at(j)], h.at[at(j)], sem.at[j])
+
+            lax.fori_loop(0, n, lambda j, c: (load(j).start(), c)[1], 0)
+            for c in ins(jnp.int32(0)):
+                c.start()
+
+            def go(j, carry):
+                load(j).wait()
+                a[at(j), :] = normed(h[at(j), :])
+                return carry
+
+            lax.fori_loop(0, n, go, 0)
+
+        def gates(g, u, p, out_sem):
+            def outs(j):
+                s = lax.rem(j, 2)
+                pairs = ((g, gate0), (u, up0), (p, p0))
+                return [pltpu.make_async_copy(src.at[s], dst.at[:, tile(j)], out_sem.at[s, i]) for i, (src, dst) in enumerate(pairs)]
+
+            def go(j, carry):
+                s = lax.rem(j, 2)
+                for c in ins(j):
+                    c.wait()
+
+                @pl.when(j < TILES - 1)
+                def _():
+                    for c in ins(j + 1):
+                        c.start()
+
+                @pl.when(j > 1)
+                def _():
+                    for c in outs(j - 2):
+                        c.wait()
+
+                for half in range(2):
+                    rows = pl.ds(half * HALF, HALF)
+                    gate, up = dot(a[rows, :], g_tile[s]), dot(a[rows, :], u_tile[s])
+                    g[s, rows, :], u[s, rows, :] = gate, up
+                    p[s, rows, :] = (gate * jax.nn.sigmoid(gate) * up).astype(BF16)
+                for c in outs(j):
+                    c.start()
+                return carry
+
+            lax.fori_loop(0, TILES, go, 0)
+            for j in (TILES - 2, TILES - 1):
+                for c in outs(jnp.int32(j)):
+                    c.wait()
+
+        def next_states(w, p, h, o, w_sem, sem, out_sem):
+            load_w = pltpu.make_async_copy(wd, w, w_sem)
+            def loads(j):
+                s = lax.rem(j, 2)
+                return [pltpu.make_async_copy(src.at[at(j, tall)], dst.at[s], sem.at[s, i]) for i, (src, dst) in enumerate(((p0, p), (x, h)))]
+
+            def out(j):
+                s = lax.rem(j, 2)
+                return pltpu.make_async_copy(o.at[s], h1.at[at(j, tall)], out_sem.at[s])
+
+            for c in (load_w, *loads(jnp.int32(0))):
+                c.start()
+            store_a.wait()
+            load_w.wait()
+
+            def go(j, carry):
+                s = lax.rem(j, 2)
+                for c in loads(j):
+                    c.wait()
+
+                @pl.when(j < n_tall - 1)
+                def _():
+                    for c in loads(j + 1):
+                        c.start()
+
+                @pl.when(j > 1)
+                def _():
+                    out(j - 2).wait()
+
+                a[at(lax.max(j - 1, 0), tall), :] = normed(o[1 - s])
+                o[s] = h[s] + dot(p[s], w[...]).astype(BF16)
+                out(j).start()
+                return carry
+
+            o[1] = jnp.zeros((tall, D), BF16)
+            lax.fori_loop(0, n_tall, go, 0)
+            a[at(n_tall - 1, tall), :] = normed(o[(n_tall - 1) % 2])
+            for j in (n_tall - 2, n_tall - 1):
+                out(jnp.int32(j)).wait()
+
+        pl.run_scoped(norm, pltpu.VMEM((T, D), BF16), pltpu.SemaphoreType.DMA((n,)))
+        store_a.start()
+        stores = [pltpu.VMEM((2, T, TILE), t) for t in (F32, F32, BF16)]
+        pl.run_scoped(gates, *stores, pltpu.SemaphoreType.DMA((2, 3)))
+        tiles = [pltpu.VMEM((FF, D), BF16), pltpu.VMEM((2, tall, FF), BF16), pltpu.VMEM((2, tall, D), BF16), pltpu.VMEM((2, tall, D), BF16)]
+        pl.run_scoped(next_states, *tiles, pltpu.SemaphoreType.DMA, pltpu.SemaphoreType.DMA((2, 2)), pltpu.SemaphoreType.DMA((2,)))
+
+    pl.run_scoped(
+        body,
+        *[pltpu.VMEM((2, D, TILE), BF16)] * 2,
+        pltpu.SemaphoreType.DMA((2, 2)),
+        pltpu.SemaphoreType.DMA,
+    )
+
+
+def last_part(tick, a, y, wg, wu, wd, dgate, dup, grads):
+    def body(g_tile, u_tile, d_tile, p, dgu, og, ou, od, in_sem, out_sem):
         dg, du = dgu.at[:, pl.ds(0, TILE)], dgu.at[:, pl.ds(TILE, TILE)]
-
-        first = [pltpu.make_async_copy(s, d, sem.at[i]) for i, (s, d) in enumerate(((a1, a), (dy, y)))]
 
         def ins(j):
             s = lax.rem(j, 2)
@@ -608,10 +700,8 @@
             pairs += ((dg, dgate.at[:, tile(j)]), (du, dup.at[:, tile(j)]))
             return [pltpu.make_async_copy(src, dst, out_sem.at[i]) for i, (src, dst) in enumerate(pairs)]
 
-        for c in first + ins(jnp.int32(0)):
+        for c in ins(jnp.int32(0)):
             c.start()
-        for c in first:
-            c.wait()
 
         def go(j, carry):
             s = lax.rem(j, 2)
@@ -657,85 +747,79 @@
     tiles = [pltpu.VMEM((2, D, TILE), BF16)] * 2 + [pltpu.VMEM((2, TILE, D), BF16)]
     pl.run_scoped(
         body,
-        *[pltpu.VMEM((T, D), BF16)] * 2,
         *tiles,
         pltpu.VMEM((T, TILE), BF16),
         pltpu.VMEM((T, 2 * TILE), BF16),
         *[pltpu.VMEM((D, TILE), BF16)] * 2,
         pltpu.VMEM((TILE, D), BF16),
-        pltpu.SemaphoreType.DMA((2,)),
         pltpu.SemaphoreType.DMA((2, 3)),
         pltpu.SemaphoreType.DMA((5,)),
     )
 
 
-def states_part(tick, dgate, dup, wg, wu, h1, dy, dh, rows=256):
+def states_part(tick, dgate, dup, wg, wu, h1, y, a, rows=256):
     n = T // rows
 
-    def body(wg_all, wu_all, dg, du, h, y, o, sem, in_sem, out_sem):
+    def body(wg_all, wu_all, dg, du, sem, in_sem):
         first = [pltpu.make_async_copy(s, d, sem.at[i]) for i, (s, d) in enumerate(((wg, wg_all), (wu, wu_all)))]
+        da = a.at[pl.ds(3 * rows, rows)]
 
         def at(j):
             return pl.ds(pl.multiple_of(j * rows, rows), rows)
 
         def ins(j):
-            s = lax.rem(j, 2)
-            pairs = ((dgate, dg), (dup, du), (h1, h), (dy, y))
-            return [pltpu.make_async_copy(src.at[at(j)], dst.at[s], in_sem.at[s, i]) for i, (src, dst) in enumerate(pairs)]
-
-        def out(j):
-            return pltpu.make_async_copy(o, dh.at[at(j)], out_sem)
-
-        for c in first + ins(jnp.int32(0)):
+            t = lax.rem(j, 3)
+            pairs = ((dgate, dg), (dup, du), (h1, a.at[at(t)]))
+            return [pltpu.make_async_copy(src.at[at(j)], dst, in_sem.at[i, t]) for i, (src, dst) in enumerate(pairs)]
+
+        def back(j, slot):
+            wide, grad = a[at(slot), :].astype(F32), da[...].astype(F32)
+            scale = lax.rsqrt(jnp.mean(wide * wide, -1, keepdims=True) + 1e-6)
+            inner = jnp.mean(grad * wide, -1, keepdims=True)
+            dh = grad * scale - wide * (scale * scale * scale * inner)
+            y[at(j), :] = (y[at(j), :].astype(F32) + dh).astype(BF16)
+
+        def ahead(j, i):
+            @pl.when(j < n - 1)
+            def _():
+                ins(j + 1)[i].start()
+
+        start = ins(jnp.int32(0))
+        for c in (start[0], first[0], start[1], first[1], start[2]):
             c.start()
+        a[pl.ds(2 * rows, 2 * rows), :] = jnp.zeros((2 * rows, D), BF16)
         for c in first:
             c.wait()
 
         def go(j, carry):
-            s = lax.rem(j, 2)
-            for c in ins(j):
-                c.wait()
-
-            @pl.when(j < n - 1)
-            def _():
-                for c in ins(j + 1):
-                    c.start()
-
-            da = (dot(dg[s], wg_all[...], NT) + dot(du[s], wu_all[...], NT)).astype(BF16).astype(F32)
-            wide = h[s].astype(F32)
-            scale = lax.rsqrt(jnp.mean(wide * wide, -1, keepdims=True) + 1e-6)
-            inner = jnp.mean(da * wide, -1, keepdims=True)
-            back = da * scale - wide * (scale * scale * scale * inner)
-
-            @pl.when(j > 0)
-            def _():
-                out(j - 1).wait()
-
-            o[...] = (y[s].astype(F32) + back).astype(BF16)
-            out(j).start()
+            here = ins(j)
+            here[2].wait()
+            ahead(j, 2)
+            here[0].wait()
+            back(lax.max(j - 1, 0), lax.rem(j + 2, 3))
+            by_gate = dot(dg[...], wg_all[...], NT)
+            ahead(j, 0)
+            here[1].wait()
+            da[...] = (by_gate + dot(du[...], wu_all[...], NT)).astype(BF16)
+            ahead(j, 1)
             tick(1, j, 0)
             return carry
 
         lax.fori_loop(0, n, go, 0)
-        out(jnp.int32(n - 1)).wait()
+        back(n - 1, (n - 1) % 3)
         tick(1, None, 0)
 
     pl.run_scoped(
         body,
         *[pltpu.VMEM((D, FF), BF16)] * 2,
-        *[pltpu.VMEM((2, rows, FF), BF16)] * 2,
-        *[pltpu.VMEM((2, rows, D), BF16)] * 2,
-        pltpu.VMEM((rows, D), BF16),
+        *[pltpu.VMEM((rows, FF), BF16)] * 2,
         pltpu.SemaphoreType.DMA((2,)),
-        pltpu.SemaphoreType.DMA((2, 4)),
-        pltpu.SemaphoreType.DMA,
+        pltpu.SemaphoreType.DMA((3, 3)),
     )
 
 
-def down0_part(tick, p0, dh, grads):
-    def body(y, p, od, sem, in_sem, out_sem):
-        first = pltpu.make_async_copy(dh, y, sem)
-
+def down0_part(tick, p0, y, grads):
+    def body(p, od, in_sem, out_sem):
         def load(j):
             s = lax.rem(j, 2)
             return pltpu.make_async_copy(p0.at[:, tile(j)], p.at[s], in_sem.at[s])
@@ -743,9 +827,7 @@
         def out(j):
             return pltpu.make_async_copy(od, grads["down"].at[tile(j)], out_sem)
 
-        first.start()
         load(jnp.int32(0)).start()
-        first.wait()
 
         def go(j, carry):
             s = lax.rem(j, 2)
@@ -770,19 +852,15 @@
 
     pl.run_scoped(
         body,
-        pltpu.VMEM((T, D), BF16),
         pltpu.VMEM((2, T, TILE), BF16),
         pltpu.VMEM((TILE, D), BF16),
-        pltpu.SemaphoreType.DMA,
         pltpu.SemaphoreType.DMA((2,)),
         pltpu.SemaphoreType.DMA,
     )
 
 
-def first_part(tick, a0, dh, wd, gate0, up0, grads):
-    def body(a, y, d_tile, g, u, dgu, og, ou, sem, in_sem, out_sem):
-        first = [pltpu.make_async_copy(s, d, sem.at[i]) for i, (s, d) in enumerate(((a0, a), (dh, y)))]
-
+def first_part(tick, a, y, wd, gate0, up0, grads):
+    def body(d_tile, g, u, dgu, og, ou, in_sem, out_sem):
         def ins(j):
             s = lax.rem(j, 2)
             pairs = ((wd.at[tile(j)], d_tile.at[s]), (gate0.at[:, tile(j)], g.at[s]), (up0.at[:, tile(j)], u.at[s]))
@@ -792,10 +870,8 @@
             pairs = ((og, grads["gate"].at[:, tile(j)]), (ou, grads["up"].at[:, tile(j)]))
             return [pltpu.make_async_copy(src, dst, out_sem.at[i]) for i, (src, dst) in enumerate(pairs)]
 
-        for c in first + ins(jnp.int32(0)):
+        for c in ins(jnp.int32(0)):
             c.start()
-        for c in first:
-            c.wait()
 
         def go(j, carry):
             s = lax.rem(j, 2)
@@ -833,40 +909,79 @@
 
     pl.run_scoped(
         body,
-        *[pltpu.VMEM((T, D), BF16)] * 2,
         pltpu.VMEM((2, TILE, D), BF16),
         *[pltpu.VMEM((2, T, TILE), F32)] * 2,
         pltpu.VMEM((T, 2 * TILE), BF16),
         *[pltpu.VMEM((D, TILE), BF16)] * 2,
-        pltpu.SemaphoreType.DMA((2,)),
         pltpu.SemaphoreType.DMA((2, 3)),
         pltpu.SemaphoreType.DMA((2,)),
     )
 
 
-def moments(sums, m, v):
+def finish(whole, sums, m, v):
+    slots, jobs = 6, 8
+
     def kernel(*refs):
-        for g, m_ref, v_ref, new_m, new_v in zip(*(refs[3 * i :][:3] for i in range(5))):
-            grad = g[...].astype(F32)
-            new_m[...] = 0.9 * m_ref[...] + 0.1 * grad
-            new_v[...] = 0.95 * v_ref[...] + 0.05 * grad * grad
-
-    shapes = [jax.ShapeDtypeStruct(t.shape, F32) for t in (*m, *v)]
-    out = pl.pallas_call(kernel, out_shape=shapes, name="moments")(*sums, *m, *v)
-    return out[:3], out[3:]
+        srcs, refs = refs[:3], refs[3:]
+        ins, outs = refs[:9], refs[9:18]
+        buffers, (in_sem, out_sem) = refs[18:20], refs[20:]
+        queue = [(i, n) for n in range(jobs) for i in range(3)]
+        used, loads, stores = [0, 0], [], []
+        for i, n in queue:
+            buffer = buffers[i // 2]
+            slot = used[i // 2] % buffer.shape[0]
+            used[i // 2] += 1
+            rows = pl.ds(n * buffer.shape[1], buffer.shape[1])
+            sems = (in_sem.at[i // 2, slot], out_sem.at[i // 2, slot])
+            loads.append(pltpu.make_async_copy(srcs[i].at[rows], buffer.at[slot], sems[0]))
+            stores.append(pltpu.make_async_copy(buffer.at[slot], outs[i].at[rows], sems[1]))
+        ahead = 2 * slots - slots // 2
+        for c in loads[:ahead]:
+            c.start()
+        for g, m_ref, v_ref, new_m, new_v in zip(*(ins[3 * i :][:3] for i in range(3)), outs[3:6], outs[6:9]):
+            for layer in range(2):
+                at = (slice(None), layer) if m_ref.shape[1] == 2 else (layer,)
+                grad = g[layer].astype(F32)
+                new_m[at] = 0.9 * m_ref[at] + 0.1 * grad
+                new_v[at] = 0.95 * v_ref[at] + 0.05 * grad * grad
+        for n, (load, store) in enumerate(zip(loads, stores)):
+            load.wait()
+            store.start()
+            if n >= 3 and n + ahead - 3 < len(loads):
+                stores[n - 3].wait()
+                loads[n + ahead - 3].start()
+        for n, store in enumerate(stores):
+            if n + ahead >= len(loads):
+                store.wait()
+
+    tall = [t.reshape(-1, t.shape[-1]) for t in whole]
+    shapes = [jax.ShapeDtypeStruct(t.shape, t.dtype) for t in (*tall, *m, *v)]
+    hbm = pl.BlockSpec(memory_space=pl.ANY)
+    vmem = pl.BlockSpec(memory_space=pltpu.VMEM)
+    buffers = [pltpu.VMEM((slots, 2 * D // jobs, FF), BF16), pltpu.VMEM((slots // 2, 2 * FF // jobs, D), BF16)]
+    out = pl.pallas_call(
+        kernel,
+        out_shape=shapes,
+        in_specs=[hbm] * 3 + [vmem] * 9,
+        out_specs=[hbm] * 3 + [vmem] * 6,
+        scratch_shapes=buffers + [pltpu.SemaphoreType.DMA((2, slots))] * 2,
+        compiler_params=pltpu.CompilerParams(vmem_limit_bytes=67043328),
+        name="finish",
+    )(*tall, *sums, *m, *v)
+    return [t.reshape(2, -1, t.shape[-1]) for t in out[:3]], out[3:6], out[6:]
+
+
+def turned(t):
+    return (*t[:2], jnp.swapaxes(t[2], 0, 1))
 
 
 def step(x, dy, *arrays):
     weights, m, v = (arrays[i : i + 3] for i in (0, 3, 6))
-    w_gate, w_up, w_down = weights
-    x, dy = x[0], dy[0]
-    me = lax.axis_index("dp")
-    blocks = [lax.dynamic_slice_in_dim(w, me * ROWS[k], ROWS[k], 1) for k, w in zip(KINDS, weights)]
-    a0, gate0, up0, p0 = gates(x, w_gate, w_up, 0)
-    h1, a1 = down(p0, w_down, x, 0)
-    whole, sums = backward(a1, h1, dy, a0, p0, gate0, up0, weights, blocks, m, v)
-    new_m, new_v = moments(sums, m, v)
-    return (*(t.reshape(2, -1, t.shape[-1]) for t in whole), *new_m, *new_v)
+    x, dy, m, v = x[0], dy[0], turned(m), turned(v)
+    block = lax.dynamic_slice_in_dim(weights[2], lax.axis_index("dp") * 22, 22, 1)
+    whole, sums = train(x, dy, weights, block, m, v)
+    new_w, new_m, new_v = finish(whole, sums, m, v)
+    return (*new_w, *turned(new_m), *turned(new_v))
 
 
 def solution(mesh):

time: 484 us -> 449 us (0.928)
  local copies, waits for them, and re-layouts: 34 us -> 1.58 us
  Pallas kernels: 443 us -> 437 us
    unnamed x15 -> x0, local copies, waits for them, and re-layouts: 30.8 us -> none
    pallas_call x4 -> x2, Pallas kernels: 443 us -> 437 us  [the longest x1 412 us: train(): pl.pallas_call(kernel, out_shape=wide + own + local, in_specs=[hbm] * 5 +...]
where the time goes in v2:
time: 449 us; the launch traced here: 440 us
  Pallas kernels  437 us (97%)
    pallas_call x1, Pallas kernels, train(): pl.pallas_call(kernel, out_shape=wide + own + local, in_specs=[hbm] * 5 +...  412 us
    pallas_call x1, Pallas kernels, finish(): pl.pallas_call(kernel, out_shape=shapes, in_specs=[hbm] * 3 + [vmem] * 9,...  25.8 us

profile of v2, /device:TPU:1, one launch (start us, length us, event | category | flops | bytes accessed | tf_op | source)
XLA Modules:
  0.0 439.8 jit_solution(9065251734915619682)
XLA Ops:
  0.6 1.6 constant_dynamic-slice_fusion.refs_5_
  2.2 411.6 %train.1 = (bf16[2,4,4,8,8,2816]{5,4,3,2,1,0:T(8,128)(2,1)}, bf16[2,4,4,8,8,2816]{5,4,3,2,1,0:T(8,128)(2,1)}, bf16[2,4,4,176,1024]{4,3,2,1,0:T(8,128)(2,1)}, bf1...) custom-call(bf16[2048,1024]{1,0:T(8,128)(2,1)} %bitcast.15, ...), custom_call_target="tpu_custom_call" | custom-call | tf_op jit(solution)/shard_map/train/pallas_call | solution.py:553
  413.8 25.8 %finish.1 = (bf16[2048,2816]{1,0:T(8,128)(2,1)}, bf16[2048,2816]{1,0:T(8,128)(2,1)}, bf16[5632,1024]{1,0:T(8,128)(2,1)}, f32[2,8,2816]{2,1,0:T(8,128)}, f32[2,8,...) custom-call(bf16[2048,2816]{1,0:T(8,128)(2,1)} %bitcast.12, ...), custom_call_target="tpu_custom_call" | custom-call | tf_op jit(solution)/shard_map/finish/pallas_call | solution.py:962

commit v3 on v2

--- a/solution.py
+++ b/solution.py
@@ -62,7 +62,7 @@
 RATE = 45.5e3
 
 
-LATENCY = 3.0
+LATENCY = 3.5
 
 
 def plan(chains, ticks, latency=LATENCY):
@@ -358,20 +358,20 @@
             return [name(what, i, *m) for m in ms]
 
         far = self.far
-        todo = [Action([], begin, listed("rs", 0, [(d, far[d]) for d in (1, -1)]), 0.06)]
+        todo = [Action([], begin, listed("rs", 0, [(d, far[d]) for d in (1, -1)]), 0.03)]
         for k in range(max(far.values()) - 1, 0, -1):
             for d in (1, -1):
                 if k < far[d]:
-                    todo.append(Action([name("rs", 0, d, k + 1)], functools.partial(add, d, k), listed("rs", 0, [(d, k)]), 0.3 if SIZE[axes[0]] == 4 else 0.13))
-        todo.append(Action(names("rs", 0, [(1, 1), (-1, 1)]), end_0, listed("rs", 1, all_of("rs", 1)), 0.4))
-        todo.append(Action(names("rs", 1, all_of("rs", 1)), end_1, listed("rs", 2, all_of("rs", 2)), 0.35))
-        todo.append(Action(names("rs", 2, all_of("rs", 2)), end_2, listed("ag", 0, all_of("ag", 0)), 0.5, True))
-        todo.append(Action(names("ag", 0, all_of("ag", 0)), functools.partial(next_back, 1), listed("ag", 1, all_of("ag", 1)), 0.25))
-        todo.append(Action(names("ag", 1, all_of("ag", 1)), functools.partial(next_back, 2), listed("ag", 2, [(1, 1), (-1, 1)]), 0.15))
+                    todo.append(Action([name("rs", 0, d, k + 1)], functools.partial(add, d, k), listed("rs", 0, [(d, k)]), 0.15 if SIZE[axes[0]] == 4 else 0.07))
+        todo.append(Action(names("rs", 0, [(1, 1), (-1, 1)]), end_0, listed("rs", 1, all_of("rs", 1)), 0.2))
+        todo.append(Action(names("rs", 1, all_of("rs", 1)), end_1, listed("rs", 2, all_of("rs", 2)), 0.2))
+        todo.append(Action(names("rs", 2, all_of("rs", 2)), end_2, listed("ag", 0, all_of("ag", 0)), 0.45, True))
+        todo.append(Action(names("ag", 0, all_of("ag", 0)), functools.partial(next_back, 1), listed("ag", 1, all_of("ag", 1)), 0.12))
+        todo.append(Action(names("ag", 1, all_of("ag", 1)), functools.partial(next_back, 2), listed("ag", 2, [(1, 1), (-1, 1)]), 0.06))
         for k in range(2, max(far.values()) + 1):
             for d in (1, -1):
                 if k <= far[d]:
-                    todo.append(Action([name("ag", 2, d, k - 1)], functools.partial(forward, d, k), listed("ag", 2, [(d, k)]), 0.1))
+                    todo.append(Action([name("ag", 2, d, k - 1)], functools.partial(forward, d, k), listed("ag", 2, [(d, k)]), 0.03))
         todo.append(Action(names("ag", 2, [(d, far[d]) for d in (1, -1)]), finish, [], 0.15))
         return todo
 
@@ -406,10 +406,10 @@
     return pl.ds(pl.multiple_of(j * TILE, TILE), TILE)
 
 
-LAST = (TILES, (4.1, 2.05, 1.4))
-STATES = (8, (4.3,))
-DOWN0 = (TILES, (1.76,))
-FIRST = (TILES, (2.24, 2.4))
+LAST = (TILES, (4.2, 2.1, 1.45))
+STATES = (8, (4.6,))
+DOWN0 = (TILES, (1.9,))
+FIRST = (TILES, (2.25, 2.45))
 PARTS = (LAST, STATES, DOWN0, FIRST)
 
 
@@ -423,20 +423,20 @@
 
 
 STRIPS = [
-    ("gate", 0, 768, 1, "zxy"),
-    ("up", 0, 768, 0, "zxy"),
-    ("gate", 768, 768, 0, "xyz"),
-    ("up", 768, 768, 0, "yxz"),
-    ("gate", 1536, 512, 1, "xyz"),
-    ("up", 1536, 512, 0, "yxz"),
-    ("gate", 2048, 512, 1, "zxy"),
-    ("up", 2048, 512, 0, "yxz"),
-    ("gate", 2560, 256, 0, "zxy"),
-    ("up", 2560, 256, 1, "zxy"),
+    ("gate", 0, 512, 1, "zxy"),
+    ("up", 0, 512, 1, "xyz"),
+    ("gate", 512, 512, 1, "zxy"),
+    ("up", 512, 512, 1, "yxz"),
+    ("gate", 1024, 768, 0, "xyz"),
+    ("up", 1024, 768, 0, "yxz"),
+    ("gate", 1792, 512, 0, "zxy"),
+    ("up", 1792, 512, 1, "yxz"),
+    ("gate", 2304, 512, 1, "zxy"),
+    ("up", 2304, 512, 0, "zxy"),
     ("down", 0, 256, 1, "yxz"),
-    ("down", 256, 256, 1, "yxz"),
-    ("down", 512, 256, 1, "xyz"),
-    ("down", 768, 256, 0, "xyz"),
+    ("down", 256, 256, 0, "yxz"),
+    ("down", 512, 256, 0, "xyz"),
+    ("down", 768, 256, 1, "xyz"),
 ]
 
 
@@ -532,8 +532,15 @@
             forward_part(x, wg.at[0], wu.at[0], wd.at[0], a0, gate0, up0, p0, h1, a)
             load.wait()
             pl.semaphore_wait(barrier, PARTNERS)
-            last_part(tick, a, y, wg.at[1], wu.at[1], wd.at[1], dgate, dup, grads[1])
-            states_part(tick, dgate, dup, wg.at[1], wu.at[1], h1, y, a)
+
+            def last_layer(w, w_sem):
+                load = pltpu.make_async_copy(wg.at[1], w, w_sem)
+                load.start()
+                last_part(tick, a, y, wg.at[1], wu.at[1], wd.at[1], dgate, dup, grads[1])
+                load.wait()
+                states_part(tick, dgate, dup, w, wu.at[1], h1, y, a)
+
+            pl.run_scoped(last_layer, pltpu.VMEM((D, FF), BF16), pltpu.SemaphoreType.DMA)
             load = pltpu.make_async_copy(a0, a, sem)
             load.start()
             down0_part(tick, p0, y, grads[0])
@@ -760,8 +767,8 @@
 def states_part(tick, dgate, dup, wg, wu, h1, y, a, rows=256):
     n = T // rows
 
-    def body(wg_all, wu_all, dg, du, sem, in_sem):
-        first = [pltpu.make_async_copy(s, d, sem.at[i]) for i, (s, d) in enumerate(((wg, wg_all), (wu, wu_all)))]
+    def body(wu_all, dg, du, sem, in_sem):
+        load_up = pltpu.make_async_copy(wu, wu_all, sem)
         da = a.at[pl.ds(3 * rows, rows)]
 
         def at(j):
@@ -785,11 +792,9 @@
                 ins(j + 1)[i].start()
 
         start = ins(jnp.int32(0))
-        for c in (start[0], first[0], start[1], first[1], start[2]):
+        for c in (start[0], load_up, start[1], start[2]):
             c.start()
         a[pl.ds(2 * rows, 2 * rows), :] = jnp.zeros((2 * rows, D), BF16)
-        for c in first:
-            c.wait()
 
         def go(j, carry):
             here = ins(j)
@@ -797,8 +802,9 @@
             ahead(j, 2)
             here[0].wait()
             back(lax.max(j - 1, 0), lax.rem(j + 2, 3))
-            by_gate = dot(dg[...], wg_all[...], NT)
+            by_gate = dot(dg[...], wg[...], NT)
             ahead(j, 0)
+            pl.when(j == 0)(load_up.wait)
             here[1].wait()
             da[...] = (by_gate + dot(du[...], wu_all[...], NT)).astype(BF16)
             ahead(j, 1)
@@ -811,9 +817,9 @@
 
     pl.run_scoped(
         body,
-        *[pltpu.VMEM((D, FF), BF16)] * 2,
+        pltpu.VMEM((D, FF), BF16),
         *[pltpu.VMEM((rows, FF), BF16)] * 2,
-        pltpu.SemaphoreType.DMA((2,)),
+        pltpu.SemaphoreType.DMA,
         pltpu.SemaphoreType.DMA((3, 3)),
     )
 
@@ -923,8 +929,10 @@
 
     def kernel(*refs):
         srcs, refs = refs[:3], refs[3:]
-        ins, outs = refs[:9], refs[9:18]
-        buffers, (in_sem, out_sem) = refs[18:20], refs[20:]
+        small, outs, refs = refs[:9], refs[9:18], refs[18:]
+        ins, results, buffers, (in_sem, out_sem, small_sem) = refs[:9], refs[9:15], refs[15:17], refs[17:]
+        brought = [pltpu.make_async_copy(src, dst, small_sem.at[n]) for n, (src, dst) in enumerate(zip(small, ins))]
+        taken = [pltpu.make_async_copy(src, dst, small_sem.at[n]) for n, (src, dst) in enumerate(zip(results, outs[3:]))]
         queue = [(i, n) for n in range(jobs) for i in range(3)]
         used, loads, stores = [0, 0], [], []
         for i, n in queue:
@@ -936,35 +944,42 @@
             loads.append(pltpu.make_async_copy(srcs[i].at[rows], buffer.at[slot], sems[0]))
             stores.append(pltpu.make_async_copy(buffer.at[slot], outs[i].at[rows], sems[1]))
         ahead = 2 * slots - slots // 2
-        for c in loads[:ahead]:
+        for c in (*loads[:3], *brought, *loads[3:ahead]):
             c.start()
-        for g, m_ref, v_ref, new_m, new_v in zip(*(ins[3 * i :][:3] for i in range(3)), outs[3:6], outs[6:9]):
-            for layer in range(2):
-                at = (slice(None), layer) if m_ref.shape[1] == 2 else (layer,)
-                grad = g[layer].astype(F32)
-                new_m[at] = 0.9 * m_ref[at] + 0.1 * grad
-                new_v[at] = 0.95 * v_ref[at] + 0.05 * grad * grad
         for n, (load, store) in enumerate(zip(loads, stores)):
             load.wait()
             store.start()
             if n >= 3 and n + ahead - 3 < len(loads):
                 stores[n - 3].wait()
                 loads[n + ahead - 3].start()
+            if n == len(loads) // 2:
+                for c in brought:
+                    c.wait()
+                for g, m_ref, v_ref, new_m, new_v in zip(*(ins[3 * i :][:3] for i in range(3)), results[:3], results[3:]):
+                    for layer in range(2):
+                        at = (slice(None), layer) if m_ref.shape[1] == 2 else (layer,)
+                        grad = g[layer].astype(F32)
+                        new_m[at] = 0.9 * m_ref[at] + 0.1 * grad
+                        new_v[at] = 0.95 * v_ref[at] + 0.05 * grad * grad
+                for c in taken:
+                    c.start()
         for n, store in enumerate(stores):
             if n + ahead >= len(loads):
                 store.wait()
+        for c in taken:
+            c.wait()
 
     tall = [t.reshape(-1, t.shape[-1]) for t in whole]
     shapes = [jax.ShapeDtypeStruct(t.shape, t.dtype) for t in (*tall, *m, *v)]
     hbm = pl.BlockSpec(memory_space=pl.ANY)
-    vmem = pl.BlockSpec(memory_space=pltpu.VMEM)
+    room = [pltpu.VMEM(t.shape, t.dtype) for t in (*sums, *m, *v, *m, *v)]
     buffers = [pltpu.VMEM((slots, 2 * D // jobs, FF), BF16), pltpu.VMEM((slots // 2, 2 * FF // jobs, D), BF16)]
     out = pl.pallas_call(
         kernel,
         out_shape=shapes,
-        in_specs=[hbm] * 3 + [vmem] * 9,
-        out_specs=[hbm] * 3 + [vmem] * 6,
-        scratch_shapes=buffers + [pltpu.SemaphoreType.DMA((2, slots))] * 2,
+        in_specs=[hbm] * 12,
+        out_specs=[hbm] * 9,
+        scratch_shapes=room + buffers + [pltpu.SemaphoreType.DMA((2, slots))] * 2 + [pltpu.SemaphoreType.DMA((9,))],
         compiler_params=pltpu.CompilerParams(vmem_limit_bytes=67043328),
         name="finish",
     )(*tall, *sums, *m, *v)

time: 449 us -> 437 us (0.973); the launches traced: 440 us -> 435 us
  Pallas kernels: 437 us -> 432 us
where the time goes in v3:
time: 437 us; the launch traced here: 435 us
  Pallas kernels  432 us (99%)
    pallas_call x1, Pallas kernels, train(): pl.pallas_call(kernel, out_shape=wide + own + local, in_specs=[hbm] * 5 +...  408 us
    pallas_call x1, Pallas kernels, finish(): pl.pallas_call(kernel, out_shape=shapes, in_specs=[hbm] * 12, out_specs=[...  23.9 us

profile of v3, /device:TPU:1, one launch (start us, length us, event | category | flops | bytes accessed | tf_op | source)
XLA Modules:
  0.0 434.8 jit_solution(9361212647321636049)
XLA Ops:
  0.6 1.6 constant_dynamic-slice_fusion.refs_5_
  2.2 408.5 %train.1 = (bf16[2,4,4,8,8,2816]{5,4,3,2,1,0:T(8,128)(2,1)}, bf16[2,4,4,8,8,2816]{5,4,3,2,1,0:T(8,128)(2,1)}, bf16[2,4,4,176,1024]{4,3,2,1,0:T(8,128)(2,1)}, bf1...) custom-call(bf16[2048,1024]{1,0:T(8,128)(2,1)} %bitcast.15, ...), custom_call_target="tpu_custom_call" | custom-call | tf_op jit(solution)/shard_map/train/pallas_call | solution.py:560
  410.7 23.9 %finish.1 = (bf16[2048,2816]{1,0:T(8,128)(2,1)}, bf16[2048,2816]{1,0:T(8,128)(2,1)}, bf16[5632,1024]{1,0:T(8,128)(2,1)}, f32[2,8,2816]{2,1,0:T(8,128)}, f32[2,8,...) custom-call(bf16[2048,2816]{1,0:T(8,128)(2,1)} %bitcast.12, ...), custom_call_target="tpu_custom_call" | custom-call | tf_op jit(solution)/shard_map/finish/pallas_call | solution.py:977
